TPU v7x, 32 devices: a whole 2x2x4 slice. The times are simulated.
32 devices in a mesh: src: 4 (over y, x), tgt: 8 (over z, core).
Axes of the slice: x: 2, y: 2, z: 4, core: 2. Of those that a mesh axis runs over, the one named last changes fastest.
Arguments:
- source_feats: bfloat16 [1, 16, 32, 1024], P(None, 'src', None, 'tgt'), may hold values from -200 to 200
- target_feats: bfloat16 [1, 32, 32, 1024], P(None, 'tgt', None, 'src'), may hold values from -200 to 200
- conv_one: bfloat16 [3, 3, 3, 3, 1, 16], replicated, may hold values from -1 to 1
- bias_one: float32 [16], replicated, may hold values from -1.5 to 1.5
- conv_two: bfloat16 [3, 3, 3, 3, 16, 16], replicated, may hold values from -0.25 to 0.25
- bias_two: float32 [16], replicated, may hold values from -1.5 to 1.5
- conv_three: bfloat16 [3, 3, 3, 3, 16, 1], replicated, may hold values from -0.25 to 0.25
- bias_three: float32 [1], replicated, may hold values from -1.5 to 1.5
Outputs:
- scores: bfloat16 [1, 16, 32, 32, 32], P(None, 'src', 'tgt')
All inputs are finite; a program needn't handle non-finite values.
Results may differ from a plain program's by a relative error of at most 0.0049.
The roundings to bfloat16 on the way count: a program that leaves them out, or rounds other values in their place, can miss the bound.
Values may be sent and summed in bfloat16 or wider, within the bound.
No kernel may reach another device: no remote copies, remote signals or barrier semaphores. Data moves between devices by JAX's collectives and lax.ppermute only.
A program may use at most 256 MiB of HBM per device.

v0:
```python
from functools import partial

import jax
import jax.numpy as jnp
from jax import lax
from jax.experimental import pallas as pl
from jax.experimental.pallas import tpu as pltpu
from jax.sharding import PartitionSpec as P

LANES = 128
TAPS = 3
HALO = 3
epsilon = 1e-06


def xor_blocks(block, axis):
    count = lax.axis_size(axis)
    blocks = block[None]
    step = 1
    while step < count:
        swap = [(i, i ^ step) for i in range(count)]
        blocks = jnp.concatenate([blocks, lax.ppermute(blocks, axis, swap)], axis=0)
        step *= 2
    return blocks


def cyclic_halo(block, axis, dim, width):
    count = lax.axis_size(axis)
    size = block.shape[dim]
    forward = [(i, (i + 1) % count) for i in range(count)]
    backward = [((i + 1) % count, i) for i in range(count)]
    low = lax.ppermute(lax.slice_in_dim(block, size - width, size, axis=dim), axis, forward)
    high = lax.ppermute(lax.slice_in_dim(block, 0, width, axis=dim), axis, backward)
    return jnp.concatenate([low, block, high], axis=dim)


def wide_blocks(blocks, axis):
    count, rows, chunk = blocks.shape
    if chunk % LANES == 0:
        return blocks, lax.axis_index(axis)
    order = lax.axis_index(axis) ^ jnp.arange(count)
    joined = jnp.take(blocks, order, axis=0).transpose(1, 0, 2).reshape(1, rows, count * chunk)
    return joined, jnp.int32(0)


def volume_kernel(pos_ref, src_ref, tgt_ref, out_ref, left_s, right_s, *, src_cols, tgt_cols):
    def normed(blocks_ref, held, index):
        count = blocks_ref.shape[0]
        squares = None
        for m in range(count):
            values = blocks_ref[m].astype(jnp.float32)
            part = jnp.sum(values * values, axis=-1, keepdims=True)
            squares = part if squares is None else squares + part
        scale = lax.rsqrt(squares + epsilon)
        for m in range(count):
            values = blocks_ref[m].astype(jnp.float32)
            held[index ^ m] = (values * scale).astype(jnp.bfloat16)
        return jnp.concatenate([held[m] for m in range(count)], axis=1)

    left = normed(src_ref, left_s, pos_ref[0])
    right = normed(tgt_ref, right_s, pos_ref[1])
    volume = lax.dot_general(
        left, right, (((1,), (1,)), ((), ())), preferred_element_type=jnp.float32
    )
    blocks = LANES // tgt_cols
    inner = src_cols // blocks
    for i in range(out_ref.shape[0]):
        for k in range(out_ref.shape[1]):
            pieces = [
                volume[
                    i * src_cols + b * inner : i * src_cols + (b + 1) * inner,
                    k * tgt_cols : (k + 1) * tgt_cols,
                ]
                for b in range(blocks)
            ]
            out_ref[i, k] = jnp.concatenate(pieces, axis=1).astype(jnp.bfloat16)


def weights_kernel(one_ref, two_ref, three_ref, w1_ref, w2_ref, w3_ref, w3_s, *, inner, rows_a, rows_b):
    channels = one_ref.shape[1]
    per_row = LANES // channels
    lane = lax.broadcasted_iota(jnp.int32, (channels, LANES), 1)
    row = lax.broadcasted_iota(jnp.int32, (channels, LANES), 0)
    lane_block = lane // channels
    spread = (lane % channels == row).astype(jnp.bfloat16)

    def tiled(ref):
        return jnp.dot(ref[...], spread, preferred_element_type=jnp.float32)

    def tap(a, b, e, g):
        return ((a * TAPS + b) * TAPS + e) * TAPS + g

    one = tiled(one_ref)
    column = jnp.where(row < inner, row, jnp.where(row == inner, inner, -2))
    column = jnp.where(row == 2 * inner - 1, -1, column)
    slabs = []
    for a in range(TAPS):
        for e in range(TAPS):
            for g in range(TAPS):
                slab = jnp.zeros((channels, LANES), jnp.float32)
                for b in range(TAPS):
                    n = tap(a, b, e, g)
                    hit = (column - lane_block == b - 1) & (column >= -1)
                    slab = jnp.where(hit, one[n : n + 1], slab)
                slabs.append(slab)
    while (len(slabs) * channels) % LANES:
        slabs.append(jnp.zeros((channels, LANES), jnp.float32))
    w1_ref[...] = jnp.concatenate(slabs, axis=0).T.astype(jnp.bfloat16)

    two = tiled(two_ref)
    for b in range(TAPS):
        for half in range(2):
            col = (b * 2 + half) * LANES
            for g in range(TAPS):
                for oi in range(2):
                    for ok in range(2):
                        block = jnp.zeros((channels, LANES), jnp.float32)
                        for low in range(2):
                            a = half * 2 + low - oi
                            if not 0 <= a < TAPS:
                                continue
                            for e in range(TAPS):
                                n = tap(a, b, e, g) * channels
                                hit = lane_block == low * 4 + ok + e
                                block = jnp.where(hit, two[n : n + channels], block)
                        at = ((g * 2 + oi) * 2 + ok) * channels
                        w2_ref[at : at + channels, col : col + LANES] = block.astype(jnp.bfloat16)

    three = tiled(three_ref)
    w3_s[...] = jnp.zeros_like(w3_s)
    lane_k = lax.broadcasted_iota(jnp.int32, (rows_b, LANES), 1) // channels
    row_k = lax.broadcasted_iota(jnp.int32, (rows_b, LANES), 0)
    for a in range(TAPS):
        for b in range(TAPS):
            for g in range(TAPS):
                block = jnp.zeros((rows_b, LANES), jnp.float32)
                for e in range(TAPS):
                    n = tap(a, b, e, g)
                    block = jnp.where(lane_k - row_k == e, three[n : n + 1], block)
                for oi in range(rows_a):
                    col = (b * (rows_a + 2) + oi + a) * LANES
                    at = (g * rows_a + oi) * rows_b
                    w3_s[at : at + rows_b, col : col + LANES] = block
    w3_ref[...] = w3_s[...].astype(jnp.bfloat16)


def layers_kernel(
    pos_ref, b3_ref, vol_ref, w1_ref, w2_ref, w3_ref, b1_ref, b2_ref, out_ref, vj, a1, a2,
    *, tgt_cols, inner, channels,
):
    ext_a, ext_b = vol_ref.shape[0], vol_ref.shape[1]
    first_a, count_a, first_b, count_b = pos_ref[0], pos_ref[1], pos_ref[2], pos_ref[3]
    wide = inner * LANES

    def inside(a, b, edge):
        ga = first_a + a - edge
        gb = first_b + b - edge
        return (ga >= 0) & (ga < count_a) & (gb >= 0) & (gb < count_b)

    def lanes(rows):
        return lax.broadcasted_iota(jnp.int32, (rows, LANES), 1)

    def up(x, step, unit, size):
        pos = lanes(x.shape[0]) % size
        return jnp.where(pos >= step, pltpu.roll(x, step, 1), 0.0)

    def down(x, step, unit, size):
        pos = lanes(x.shape[0]) % size
        return jnp.where(pos < size - step, pltpu.roll(x, LANES - step, 1), 0.0)

    plane_row = lax.broadcasted_iota(jnp.int32, (inner, LANES), 0)

    def spread_row(a, carry):
        for b in range(ext_b):
            x = vol_ref[a, b].astype(jnp.float32)
            x = jnp.where(inside(a, b, HALO), x, 0.0)
            before = up(x, tgt_cols, 0, LANES)
            after = down(x, tgt_cols, 0, LANES)
            edge = jnp.where(plane_row == inner - 1, before, jnp.where(plane_row == 0, after, 0.0))
            both = jnp.concatenate([x, edge], axis=0)
            rows = 2 * inner
            vj[a, b, 0:rows] = up(both, 1, 0, tgt_cols).astype(jnp.bfloat16)
            vj[a, b, rows : 2 * rows] = both.astype(jnp.bfloat16)
            vj[a, b, 2 * rows : 3 * rows] = down(both, 1, 0, tgt_cols).astype(jnp.bfloat16)
        return carry

    lax.fori_loop(0, ext_a, spread_row, 0)

    def put(dst, a, b, blocks):
        dst[a, b, 0:channels] = up(blocks[-1], tgt_cols, 0, LANES).astype(jnp.bfloat16)
        for n, block in enumerate(blocks):
            dst[a, b, (n + 1) * channels : (n + 2) * channels] = block.astype(jnp.bfloat16)
        dst[a, b, (inner + 1) * channels :] = down(blocks[0], tgt_cols, 0, LANES).astype(jnp.bfloat16)

    l1_a, l1_b = ext_a - 2, ext_b - 2
    bias1 = jnp.broadcast_to(b1_ref[...], (channels, LANES))
    depth1 = TAPS * TAPS * TAPS * 2 * inner
    group = 4 if l1_b % 4 == 0 else 2

    def first_row(a, carry):
        for b0 in range(0, l1_b, group):
            x = jnp.concatenate(
                [
                    jnp.concatenate(
                        [vj[a + da, b0 + n + db] for da in range(TAPS) for db in range(TAPS)], axis=0
                    )
                    for n in range(group)
                ],
                axis=1,
            )
            got = jnp.dot(w1_ref[:, :depth1], x, preferred_element_type=jnp.float32)
            for n in range(group):
                ok = inside(a, b0 + n, HALO - 1)
                blocks = [
                    jnp.where(
                        ok,
                        jnp.maximum(
                            got[c * channels : (c + 1) * channels, n * LANES : (n + 1) * LANES]
                            + bias1,
                            0.0,
                        ),
                        0.0,
                    )
                    for c in range(inner)
                ]
                put(a1, a, b0 + n, blocks)
        return carry

    lax.fori_loop(0, l1_a, first_row, 0)

    l2_a, l2_b = l1_a - 2, l1_b - 2
    bias2 = jnp.broadcast_to(b2_ref[...], (channels, LANES))
    cells = 4 * channels
    half = inner // 2

    for a in range(l2_a):
        for b in range(l2_b, a2.shape[1]):
            a2[a, b] = jnp.zeros(a2.shape[2:], jnp.bfloat16)

    def second_patch(n, carry):
        pa = (n // (l2_b // 2)) * 2
        pb = (n % (l2_b // 2)) * 2
        for h in range(2):
            x = jnp.concatenate(
                [
                    jnp.concatenate(
                        [
                            a1[pa + wi, pb + wk, (c + dj) * channels : (c + dj + 1) * channels]
                            for dj in range(TAPS)
                            for wi in range(4)
                            for wk in range(4)
                        ],
                        axis=0,
                    )
                    for c in range(h * half, (h + 1) * half)
                ],
                axis=1,
            )
            got = jnp.dot(w2_ref[...], x, preferred_element_type=jnp.float32)
            for q in range(half):
                part = got[:, q * LANES : (q + 1) * LANES]
                total = (
                    part[cells : 2 * cells]
                    + up(part[:cells], 1, 0, tgt_cols)
                    + down(part[2 * cells :], 1, 0, tgt_cols)
                )
                c = h * half + q
                for oi in range(2):
                    for ok in range(2):
                        at = (oi * 2 + ok) * channels
                        block = jnp.maximum(total[at : at + channels] + bias2, 0.0)
                        block = jnp.where(inside(pa + oi, pb + ok, HALO - 2), block, 0.0)
                        a2[pa + oi, pb + ok, (c + 1) * channels : (c + 2) * channels] = block.astype(
                            jnp.bfloat16
                        )
                        if c == inner - 1:
                            a2[pa + oi, pb + ok, 0:channels] = up(block, tgt_cols, 0, LANES).astype(
                                jnp.bfloat16
                            )
                        if c == 0:
                            a2[pa + oi, pb + ok, (inner + 1) * channels :] = down(
                                block, tgt_cols, 0, LANES
                            ).astype(jnp.bfloat16)
        return carry

    lax.fori_loop(0, (l2_a // 2) * (l2_b // 2), second_patch, 0)

    cells = out_ref.shape[0]
    for h in range(2):
        x = jnp.concatenate(
            [
                jnp.concatenate(
                    [
                        a2[wi, wk, (c + dj) * channels : (c + dj + 1) * channels]
                        for dj in range(TAPS)
                        for wi in range(l2_a)
                        for wk in range(a2.shape[1])
                    ],
                    axis=0,
                )
                for c in range(h * half, (h + 1) * half)
            ],
            axis=1,
        )
        got = jnp.dot(w3_ref[...], x, preferred_element_type=jnp.float32)
        for q in range(half):
            part = got[:, q * LANES : (q + 1) * LANES]
            total = (
                part[cells : 2 * cells]
                + up(part[:cells], 1, 0, tgt_cols)
                + down(part[2 * cells :], 1, 0, tgt_cols)
            )
            c = h * half + q
            out_ref[:, c * LANES : (c + 1) * LANES] = jnp.maximum(total + b3_ref[0], 0.0).astype(
                jnp.bfloat16
            )


VMEM = pl.BlockSpec(memory_space=pltpu.VMEM)
SMEM = pl.BlockSpec(memory_space=pltpu.SMEM)


def one_pair(source, target, conv_one, bias_one, conv_two, bias_two, conv_three, bias_three):
    rows_a, src_cols, _ = source.shape
    rows_b, tgt_cols, _ = target.shape
    channels = conv_two.shape[-1]
    blocks = LANES // tgt_cols
    inner = src_cols // blocks
    assert 2 * inner == channels and LANES % tgt_cols == 0
    assert rows_a % 2 == 0 and rows_b % 2 == 0 and min(rows_a, rows_b) >= HALO

    left = xor_blocks(source.reshape(rows_a * src_cols, -1), "tgt")
    right = xor_blocks(target.reshape(rows_b * tgt_cols, -1), "src")
    left, left_at = wide_blocks(left, "tgt")
    right, right_at = wide_blocks(right, "src")

    taps = TAPS**4
    w3_cols = TAPS * (rows_a + 2) * LANES
    w1_cols = -(-(TAPS**3 * channels) // LANES) * LANES
    w1, w2, w3 = pl.pallas_call(
        partial(weights_kernel, inner=inner, rows_a=rows_a, rows_b=rows_b),
        out_shape=(
            jax.ShapeDtypeStruct((LANES, w1_cols), jnp.bfloat16),
            jax.ShapeDtypeStruct((TAPS * 4 * channels, TAPS * 2 * LANES), jnp.bfloat16),
            jax.ShapeDtypeStruct((TAPS * rows_a * rows_b, w3_cols), jnp.bfloat16),
        ),
        in_specs=[VMEM] * 3,
        out_specs=(VMEM, VMEM, VMEM),
        scratch_shapes=[pltpu.VMEM((TAPS * rows_a * rows_b, w3_cols), jnp.float32)],
        cost_estimate=pl.CostEstimate(flops=2_000_000_000, bytes_accessed=1_000_000, transcendentals=0),
        name="weights",
    )(
        conv_one.reshape(taps, channels),
        conv_two.reshape(taps, channels, channels).swapaxes(1, 2).reshape(taps * channels, channels),
        conv_three.reshape(taps, channels),
    )

    volume = pl.pallas_call(
        partial(volume_kernel, src_cols=src_cols, tgt_cols=tgt_cols),
        out_shape=jax.ShapeDtypeStruct((rows_a, rows_b, inner, LANES), jnp.bfloat16),
        in_specs=[SMEM, VMEM, VMEM],
        out_specs=VMEM,
        scratch_shapes=[pltpu.VMEM(left.shape, jnp.bfloat16), pltpu.VMEM(right.shape, jnp.bfloat16)],
        name="volume",
    )(jnp.stack([left_at, right_at]).astype(jnp.int32), left, right)

    volume = cyclic_halo(volume, "src", 0, HALO)
    volume = cyclic_halo(volume, "tgt", 1, HALO)
    ext_a, ext_b = rows_a + 2 * HALO, rows_b + 2 * HALO
    place = jnp.stack(
        [
            lax.axis_index("src") * rows_a,
            lax.axis_size("src") * rows_a,
            lax.axis_index("tgt") * rows_b,
            lax.axis_size("tgt") * rows_b,
        ]
    ).astype(jnp.int32)
    wide_b = LANES // channels
    scores = pl.pallas_call(
        partial(layers_kernel, tgt_cols=tgt_cols, inner=inner, channels=channels),
        out_shape=jax.ShapeDtypeStruct((rows_a * rows_b, inner * LANES), jnp.bfloat16),
        in_specs=[SMEM, SMEM] + [VMEM] * 6,
        out_specs=VMEM,
        scratch_shapes=[
            pltpu.VMEM((ext_a, ext_b, TAPS * 2 * inner, LANES), jnp.bfloat16),
            pltpu.VMEM((ext_a - 2, ext_b - 2, (inner + 2) * channels, LANES), jnp.bfloat16),
            pltpu.VMEM((ext_a - 4, wide_b, (inner + 2) * channels, LANES), jnp.bfloat16),
        ],
        name="layers",
    )(place, bias_three, volume, w1, w2, w3, bias_one[:, None], bias_two[:, None])
    scores = scores.reshape(rows_a, rows_b, inner, blocks, tgt_cols).transpose(0, 1, 3, 2, 4)
    return scores.reshape(rows_a, rows_b, src_cols, tgt_cols)


def local(source_feats, target_feats, *params):
    return jnp.stack(
        [one_pair(source_feats[p], target_feats[p], *params) for p in range(source_feats.shape[0])]
    )


def solution(mesh):
    return jax.shard_map(
        local,
        mesh=mesh,
        in_specs=(
            P(None, "src", None, "tgt"),
            P(None, "tgt", None, "src"),
            P(),
            P(),
            P(),
            P(),
            P(),
            P(),
        ),
        out_specs=P(None, "src", "tgt", None, None),
        check_vma=False,
    )
```

profile of v0, /device:TPU:0, one launch (start us, length us, event | category | flops | bytes accessed | tf_op | source)
XLA Modules:
  0.0 51.0 jit_solution(8425101842988884013)
XLA Ops:
  0.0 0.5 collective-permute-start
  0.5 2.5 %collective-permute-start.3 = (bf16[1,128,256]{2,1,0:T(8,128)(2,1)}, bf16[1,128,256]{2,1,0:T(8,128)(2,1)S(1)}, u32[]{:S(2)}, u32[]{:S(2)}) collective-permute-start(bf16[1,128,256]{2,1,0:T(8,128)(2,1)} %bitcast.27), channel_id=1, source_target_pairs={{0,8},{8,0},{16,24},{24,16},{1,9},{9,1},{17,25},{25,17},{2,10},{10... | collective-permute-start | bytes 196616 | tf_op jit(solution)/shard_map/ppermute | solution.py:22
  3.0 0.0 copy-start.1
  3.0 0.0 collective-permute-done
  3.0 0.8 %pad_maximum_fusion.6 = bf16[2,128,128]{2,1,0:T(8,128)(2,1)S(1)} fusion(bf16[1,128,128]{2,1,0:T(8,128)(2,1)S(1)} %collective-permute-done, bf16[1,128,128]{2,1,0:T(8,128)(2,1)} %bitcast.24), kind=kLoop, calls=%fused_computation.7 | loop fusion | flops 32768 | bytes 131072 | tf_op jit(solution)/shard_map/concatenate | solution.py:22
  3.8 0.0 copy-start.2
  3.8 1.6 %collective-permute-start.1 = (bf16[2,128,128]{2,1,0:T(8,128)(2,1)S(1)}, bf16[2,128,128]{2,1,0:T(8,128)(2,1)S(1)}, u32[]{:S(2)}, u32[]{:S(2)}) collective-permute-start(bf16[2,128,128]{2,1,0:T(8,128)(2,1)S(1)} %pad_maximum_fusion.6), channel_id=1, source_target_pairs={{0,2},{1,3},{2,0},{3,1},{4,6},{5,7},{6,4},{7,5},{8,10},{9,11},{10,... | collective-permute-start | bytes 196616 | tf_op jit(solution)/shard_map/ppermute | solution.py:22
  5.4 0.5 collective-permute-done.3
  5.9 0.9 %pad_maximum_fusion.4 = bf16[2,128,256]{2,1,0:T(8,128)(2,1)S(1)} fusion(bf16[1,128,256]{2,1,0:T(8,128)(2,1)S(1)} %collective-permute-done.3, bf16[1,128,256]{2,1,0:T(8,128)(2,1)} %bitcast.28), kind=kLoop, calls=%fused_computation.4 | loop fusion | flops 65536 | bytes 262144 | tf_op jit(solution)/shard_map/concatenate | solution.py:22
  6.8 1.8 %collective-permute-start.4 = (bf16[2,128,256]{2,1,0:T(8,128)(2,1)S(1)}, bf16[2,128,256]{2,1,0:T(8,128)(2,1)S(1)}, u32[]{:S(2)}, u32[]{:S(2)}) collective-permute-start(bf16[2,128,256]{2,1,0:T(8,128)(2,1)S(1)} %pad_maximum_fusion.4), channel_id=1, source_target_pairs={{0,16},{8,24},{16,0},{24,8},{1,17},{9,25},{17,1},{25,9},{2,18},{10... | collective-permute-start | bytes 393224 | tf_op jit(solution)/shard_map/ppermute | solution.py:22
  8.6 0.0 collective-permute-done.1
  8.6 0.0 copy-done.2
  8.7 2.7 %collective-permute-start.2 = (bf16[4,128,128]{2,1,0:T(8,128)(2,1)S(1)}, bf16[4,128,128]{2,1,0:T(8,128)(2,1)S(1)}, u32[]{:S(2)}, u32[]{:S(2)}) collective-permute-start(bf16[4,128,128]{2,1,0:T(8,128)(2,1)S(1)} %pad_maximum_fusion.3), channel_id=1, source_target_pairs={{0,4},{1,5},{2,6},{3,7},{4,0},{5,1},{6,2},{7,3},{8,12},{9,13},{10,... | collective-permute-start | bytes 393224 | tf_op jit(solution)/shard_map/ppermute | solution.py:22
  11.3 0.6 %pad_add_fusion.1.pos_ref = s32[2]{0:T(128)} fusion(s32[1]{0:T(128)} %bitcast.3, s32[1]{0:T(128)} %bitcast.2), kind=kLoop, calls=%fused_computation.9 | loop fusion | flops 2 | bytes 16 | tf_op jit(solution)/shard_map/stack | solution.py:365
  11.9 0.0 copy-done.1
  11.9 0.0 copy-start.4
  11.9 0.0 copy-start.5
  11.9 0.9 %copy.13 = bf16[81,16,16]{1,2,0:T(8,128)(2,1)} copy(bf16[81,16,16]{2,1,0:T(8,128)(2,1)S(1)} %bitcast.21) | data formatting | bytes 82944 | tf_op jit(solution)/shard_map/reshape | solution.py:354
  12.8 0.0 copy-done.4
  12.8 0.0 copy-start.3
  12.8 0.6 %reshape.15.one_ref = bf16[81,16]{1,0:T(8,128)(2,1)} reshape(bf16[3,3,3,3,1,16]{5,3,4,2,1,0:T(4,128)(2,1)S(1)} %copy-done.4) | data formatting | bytes 5184 | tf_op jit(solution)/shard_map/reshape | solution.py:353
  13.4 0.0 copy-done.5
  13.4 0.6 %reshape.18.three_ref = bf16[81,16]{1,0:T(8,128)(2,1)} reshape(bf16[3,3,3,3,16,1]{4,3,5,2,1,0:T(4,128)(2,1)S(1)} %copy-done.5) | data formatting | bytes 5184 | tf_op jit(solution)/shard_map/reshape | solution.py:355
  14.1 0.0 collective-permute-done.4
  14.1 0.0 copy-done.3
  14.1 0.7 %pad_maximum_fusion.1.tgt_ref = bf16[4,128,256]{2,1,0:T(8,128)(2,1)} fusion(bf16[2,128,256]{2,1,0:T(8,128)(2,1)S(1)} %collective-permute-done.4, bf16[1,128,256]{2,1,0:T(8,128)(2,1)S(1)} %collective-permute-done.3, bf16[1,128,256]{2,1,0:T(8,128)(2,1)S(1)} %bitcast.29), kind=kLoop, calls=%fused_computation.1 | loop fusion | flops 262144 | bytes 524288 | tf_op jit(solution)/shard_map/concatenate | solution.py:22
  14.8 2.4 %collective-permute-done.2 = bf16[4,128,128]{2,1,0:T(8,128)(2,1)S(1)} collective-permute-done((bf16[4,128,128]{2,1,0:T(8,128)(2,1)S(1)}, bf16[4,128,128]{2,1,0:T(8,128)(2,1)S(1)}, u32[]{:S(2)}, u32[]{:S(2)}) %collective-permute-start.2) | collective-permute-done | bytes 131104 | tf_op jit(solution)/shard_map/ppermute | solution.py:22
  17.2 0.7 %pad_maximum_fusion.src_ref = bf16[8,128,128]{2,1,0:T(8,128)(2,1)} fusion(bf16[4,128,128]{2,1,0:T(8,128)(2,1)S(1)} %collective-permute-done.2, bf16[2,128,128]{2,1,0:T(8,128)(2,1)S(1)} %collective-permute-done.1, bf16[1,128,128]{2,1,0:T(8,128)(2,1)S(1)} %collective-permute-done, bf16[1,128,128]{2,1,0:T(8,128)(2,1)S(1)} %bitcast.26), kind=kLoop, calls=%fused_computation | loop fusion | flops 393216 | bytes 524288 | tf_op jit(solution)/shard_map/concatenate | solution.py:22
  17.9 2.3 %volume.1 = bf16[4,4,8,128]{3,2,1,0:T(8,128)(2,1)} custom-call(s32[2]{0:T(128)} %pad_add_fusion.1.pos_ref, bf16[8,128,128]{2,1,0:T(8,128)(2,1)} %pad_maximum_fusion.src_ref, bf16[4,128,256]{2,1,0:T(8,128)(2,1)} %pad_maximum_fusion.1.tgt_ref), custom_call_target="tpu_custom_call" | custom-call | tf_op jit(solution)/shard_map/volume/pallas_call | solution.py:358
  20.2 0.8 %fusion.1 = (bf16[3,4,8,128]{3,2,1,0:T(8,128)(2,1)S(1)}, bf16[3,4,8,128]{3,2,1,0:T(8,128)(2,1)S(1)}) fusion(bf16[4,4,8,128]{3,2,1,0:T(8,128)(2,1)} %volume.1), kind=kLoop, calls=%fused_computation.11 | loop fusion | bytes 98304 | tf_op jit(solution)/shard_map/slice | solution.py:32
  21.0 1.5 %collective-permute-start.5 = (bf16[3,4,8,128]{3,2,1,0:T(8,128)(2,1)S(1)}, bf16[3,4,8,128]{3,2,1,0:T(8,128)(2,1)S(1)}, u32[]{:S(2)}, u32[]{:S(2)}) collective-permute-start(bf16[3,4,8,128]{3,2,1,0:T(8,128)(2,1)S(1)} %get-tuple-element.13), channel_id=1, source_target_pairs={{0,8},{8,16},{16,24},{24,0},{1,9},{9,17},{17,25},{25,1},{2,10},{10... | collective-permute-start | bytes 73736 | tf_op jit(solution)/shard_map/ppermute | solution.py:32
  22.5 1.4 %collective-permute-start.6 = (bf16[3,4,8,128]{3,2,1,0:T(8,128)(2,1)S(1)}, bf16[3,4,8,128]{3,2,1,0:T(8,128)(2,1)S(1)}, u32[]{:S(2)}, u32[]{:S(2)}) collective-permute-start(bf16[3,4,8,128]{3,2,1,0:T(8,128)(2,1)S(1)} %get-tuple-element.14), channel_id=1, source_target_pairs={{8,0},{16,8},{24,16},{0,24},{9,1},{17,9},{25,17},{1,25},{10,2},{18... | collective-permute-start | bytes 73736 | tf_op jit(solution)/shard_map/ppermute | solution.py:33
  23.9 0.0 copy-start
  23.9 2.2 %weights.1 = (bf16[128,512]{1,0:T(8,128)(2,1)}, bf16[192,768]{1,0:T(8,128)(2,1)}, bf16[48,2304]{1,0:T(8,128)(2,1)}) custom-call(bf16[81,16]{1,0:T(8,128)(2,1)} %reshape.15.one_ref, bf16[1296,16]{1,0:T(8,128)(2,1)} %bitcast.22, bf16[81,16]{1,0:T(8,128)(2,1)} %reshape.18.three_ref), custom_call_target="tpu_custom_call" | custom-call | flops 2000000000 | bytes 1000000 | tf_op jit(solution)/shard_map/weights/pallas_call | solution.py:340
  26.1 0.0 copy-start.6
  26.1 0.7 %copy-done.6 = f32[16]{0:T(128)S(1)} copy-done((f32[16]{0:T(128)S(1)}, f32[16]{0:T(128)}, u32[]{:S(2)}) %copy-start.6) | copy-done | bytes 88
  26.8 0.7 %copy.14.b1_ref = f32[16,1]{1,0:T(8,128)} copy(f32[16,1]{0,1:T(1,128)S(1)} %bitcast.30) | data formatting | bytes 128 | tf_op jit(solution)/shard_map/broadcast_in_dim | solution.py:390
  27.5 0.0 copy-start.7
  27.5 0.7 %copy-done.7 = f32[16]{0:T(128)S(1)} copy-done((f32[16]{0:T(128)S(1)}, f32[16]{0:T(128)}, u32[]{:S(2)}) %copy-start.7) | copy-done | bytes 88
  28.1 0.7 %copy.15.b2_ref = f32[16,1]{1,0:T(8,128)} copy(f32[16,1]{0,1:T(1,128)S(1)} %bitcast.31) | data formatting | bytes 128 | tf_op jit(solution)/shard_map/broadcast_in_dim | solution.py:390
  29.5 0.0 collective-permute-done.5
  29.5 0.0 collective-permute-done.6
  29.5 0.0 copy-done
  29.5 0.1 collective-permute-start.7
  29.6 3.5 %collective-permute-start.8 = (bf16[10,3,8,128]{3,2,1,0:T(8,128)(2,1)S(1)}, bf16[10,3,8,128]{3,2,1,0:T(8,128)(2,1)S(1)}, u32[]{:S(2)}, u32[]{:S(2)}) collective-permute-start(bf16[10,3,8,128]{3,2,1,0:T(8,128)(2,1)S(1)} %get-tuple-element.12), channel_id=1, source_target_pairs={{1,0},{2,1},{3,2},{4,3},{5,4},{6,5},{7,6},{0,7},{9,8},{10,9},{11,1... | collective-permute-start | bytes 184328 | tf_op jit(solution)/shard_map/ppermute | solution.py:33
  33.1 0.7 %pad_add_fusion.pos_ref = s32[4]{0:T(128)} fusion(s32[1]{0:T(128)} %constant.13.clone.1, s32[1]{0:T(128)} %bitcast.1, s32[1]{0:T(128)} %constant.4.clone.1, s32[1]{0:T(128)} %bitcast), kind=kLoop, calls=%fused_computation.8 | loop fusion | flops 12 | bytes 32 | tf_op jit(solution)/shard_map/stack | solution.py:370
  33.8 1.2 %collective-permute-done.7 = bf16[10,3,8,128]{3,2,1,0:T(8,128)(2,1)S(1)} collective-permute-done((bf16[10,3,8,128]{3,2,1,0:T(8,128)(2,1)S(1)}, bf16[10,3,8,128]{3,2,1,0:T(8,128)(2,1)S(1)}, u32[]{:S(2)}, u32[]{:S(2)}) %collective-permute-start.7) | collective-permute-done | bytes 61472 | tf_op jit(solution)/shard_map/ppermute | solution.py:32
  35.0 0.0 collective-permute-done.8
  35.0 0.7 %pad_maximum_fusion.2.vol_ref = bf16[10,10,8,128]{3,2,1,0:T(8,128)(2,1)} fusion(bf16[10,3,8,128]{3,2,1,0:T(8,128)(2,1)S(1)} %collective-permute-done.8, bf16[3,4,8,128]{3,2,1,0:T(8,128)(2,1)S(1)} %collective-permute-done.6, bf16[4,4,8,128]{3,2,1,0:T(8,128)(2,1)S(1)} %copy-done, bf16[3,4,8,128]{3,2,1,0:T(8,128)(2,1)S(1)} %collective-permute-done.5, ...), kind=kLoop, calls=%fused_computation.2 | loop fusion | flops 409600 | bytes 409600 | tf_op jit(solution)/shard_map/concatenate | solution.py:34
  35.7 13.6 %layers.1 = bf16[16,1024]{1,0:T(8,128)(2,1)} custom-call(s32[4]{0:T(128)} %pad_add_fusion.pos_ref, f32[1]{0:T(128)S(6)} %copy.19.b3_ref, bf16[10,10,8,128]{3,2,1,0:T(8,128)(2,1)} %pad_maximum_fusion.2.vol_ref, bf16[128,512]{1,0:T(8,128)(2,1)} %get-tuple-element.8.w1_ref, bf16[192,768]{1,0:T(8,128)(2,1)} %get-tuple-element.9.w2_ref, ...), custom_call_target="tpu_custom_call" | custom-call | tf_op jit(solution)/shard_map/layers/pallas_call | solution.py:379
  49.4 0.9 %reshape.19 = bf16[4,4,8,4,32]{4,3,2,1,0:T(4,128)(2,1)S(1)} reshape(bf16[16,1024]{1,0:T(8,128)(2,1)} %layers.1) | data formatting | bytes 65536 | tf_op jit(solution)/shard_map/reshape | solution.py:391
  50.3 0.7 %copy.18 = bf16[4,4,4,8,32]{4,3,2,1,0:T(8,128)(2,1)} copy(bf16[4,4,4,8,32]{4,2,3,1,0:T(4,128)(2,1)S(1)} %bitcast.20) | data formatting | bytes 65536 | tf_op jit(solution)/shard_map/transpose | solution.py:391
  (3 shorter events, 0.0 us)
Async XLA Ops:
  0.0 3.0 %collective-permute-start = (bf16[1,128,128]{2,1,0:T(8,128)(2,1)}, bf16[1,128,128]{2,1,0:T(8,128)(2,1)S(1)}, u32[]{:S(2)}, u32[]{:S(2)}) collective-permute-start(bf16[1,128,128]{2,1,0:T(8,128)(2,1)} %bitcast.23), channel_id=1, source_target_pairs={{0,1},{1,0},{2,3},{3,2},{4,5},{5,4},{6,7},{7,6},{8,9},{9,8},{10,11... | collective-permute-start | bytes 98312 | tf_op jit(solution)/shard_map/ppermute | solution.py:22
  0.5 5.4 %collective-permute-start.3 = (bf16[1,128,256]{2,1,0:T(8,128)(2,1)}, bf16[1,128,256]{2,1,0:T(8,128)(2,1)S(1)}, u32[]{:S(2)}, u32[]{:S(2)}) collective-permute-start(bf16[1,128,256]{2,1,0:T(8,128)(2,1)} %bitcast.27), channel_id=1, source_target_pairs={{0,8},{8,0},{16,24},{24,16},{1,9},{9,1},{17,25},{25,17},{2,10},{10... | collective-permute-start | bytes 196616 | tf_op jit(solution)/shard_map/ppermute | solution.py:22
  3.0 8.9 %copy-start.1 = (bf16[3,3,3,3,16,16]{5,4,3,2,1,0:T(8,128)(2,1)S(1)}, bf16[3,3,3,3,16,16]{5,4,3,2,1,0:T(8,128)(2,1)}, u32[]{:S(2)}) copy-start(bf16[3,3,3,3,16,16]{5,4,3,2,1,0:T(8,128)(2,1)} %param.12) | copy-start | bytes 124420
  3.8 4.9 %copy-start.2 = (bf16[1,4,32,128]{3,2,1,0:T(8,128)(2,1)S(1)}, bf16[1,4,32,128]{3,2,1,0:T(8,128)(2,1)}, u32[]{:S(2)}) copy-start(bf16[1,4,32,128]{3,2,1,0:T(8,128)(2,1)} %param.8) | copy-start | bytes 98308
  3.8 4.8 %collective-permute-start.1 = (bf16[2,128,128]{2,1,0:T(8,128)(2,1)S(1)}, bf16[2,128,128]{2,1,0:T(8,128)(2,1)S(1)}, u32[]{:S(2)}, u32[]{:S(2)}) collective-permute-start(bf16[2,128,128]{2,1,0:T(8,128)(2,1)S(1)} %pad_maximum_fusion.6), channel_id=1, source_target_pairs={{0,2},{1,3},{2,0},{3,1},{4,6},{5,7},{6,4},{7,5},{8,10},{9,11},{10,... | collective-permute-start | bytes 196616 | tf_op jit(solution)/shard_map/ppermute | solution.py:22
  6.8 7.3 %collective-permute-start.4 = (bf16[2,128,256]{2,1,0:T(8,128)(2,1)S(1)}, bf16[2,128,256]{2,1,0:T(8,128)(2,1)S(1)}, u32[]{:S(2)}, u32[]{:S(2)}) collective-permute-start(bf16[2,128,256]{2,1,0:T(8,128)(2,1)S(1)} %pad_maximum_fusion.4), channel_id=1, source_target_pairs={{0,16},{8,24},{16,0},{24,8},{1,17},{9,25},{17,1},{25,9},{2,18},{10... | collective-permute-start | bytes 393224 | tf_op jit(solution)/shard_map/ppermute | solution.py:22
  8.7 8.5 %collective-permute-start.2 = (bf16[4,128,128]{2,1,0:T(8,128)(2,1)S(1)}, bf16[4,128,128]{2,1,0:T(8,128)(2,1)S(1)}, u32[]{:S(2)}, u32[]{:S(2)}) collective-permute-start(bf16[4,128,128]{2,1,0:T(8,128)(2,1)S(1)} %pad_maximum_fusion.3), channel_id=1, source_target_pairs={{0,4},{1,5},{2,6},{3,7},{4,0},{5,1},{6,2},{7,3},{8,12},{9,13},{10,... | collective-permute-start | bytes 393224 | tf_op jit(solution)/shard_map/ppermute | solution.py:22
  11.9 0.9 %copy-start.4 = (bf16[3,3,3,3,1,16]{5,3,4,2,1,0:T(4,128)(2,1)S(1)}, bf16[3,3,3,3,1,16]{5,3,4,2,1,0:T(4,128)(2,1)}, u32[]{:S(2)}) copy-start(bf16[3,3,3,3,1,16]{5,3,4,2,1,0:T(4,128)(2,1)} %param.10) | copy-start | bytes 7780
  11.9 1.5 %copy-start.5 = (bf16[3,3,3,3,16,1]{4,3,5,2,1,0:T(4,128)(2,1)S(1)}, bf16[3,3,3,3,16,1]{4,3,5,2,1,0:T(4,128)(2,1)}, u32[]{:S(2)}) copy-start(bf16[3,3,3,3,16,1]{4,3,5,2,1,0:T(4,128)(2,1)} %param.14) | copy-start | bytes 7780
  12.8 1.3 %copy-start.3 = (bf16[1,4,32,256]{3,2,1,0:T(8,128)(2,1)S(1)}, bf16[1,4,32,256]{3,2,1,0:T(8,128)(2,1)}, u32[]{:S(2)}) copy-start(bf16[1,4,32,256]{3,2,1,0:T(8,128)(2,1)} %param.9) | copy-start | bytes 196612
  21.0 8.4 %collective-permute-start.5 = (bf16[3,4,8,128]{3,2,1,0:T(8,128)(2,1)S(1)}, bf16[3,4,8,128]{3,2,1,0:T(8,128)(2,1)S(1)}, u32[]{:S(2)}, u32[]{:S(2)}) collective-permute-start(bf16[3,4,8,128]{3,2,1,0:T(8,128)(2,1)S(1)} %get-tuple-element.13), channel_id=1, source_target_pairs={{0,8},{8,16},{16,24},{24,0},{1,9},{9,17},{17,25},{25,1},{2,10},{10... | collective-permute-start | bytes 73736 | tf_op jit(solution)/shard_map/ppermute | solution.py:32
  22.5 7.0 %collective-permute-start.6 = (bf16[3,4,8,128]{3,2,1,0:T(8,128)(2,1)S(1)}, bf16[3,4,8,128]{3,2,1,0:T(8,128)(2,1)S(1)}, u32[]{:S(2)}, u32[]{:S(2)}) collective-permute-start(bf16[3,4,8,128]{3,2,1,0:T(8,128)(2,1)S(1)} %get-tuple-element.14), channel_id=1, source_target_pairs={{8,0},{16,8},{24,16},{0,24},{9,1},{17,9},{25,17},{1,25},{10,2},{18... | collective-permute-start | bytes 73736 | tf_op jit(solution)/shard_map/ppermute | solution.py:33
  23.9 5.5 %copy-start = (bf16[4,4,8,128]{3,2,1,0:T(8,128)(2,1)S(1)}, bf16[4,4,8,128]{3,2,1,0:T(8,128)(2,1)}, u32[]{:S(2)}) copy-start(bf16[4,4,8,128]{3,2,1,0:T(8,128)(2,1)} %volume.1) | copy-start | bytes 98308
  26.1 0.7 %copy-start.6 = (f32[16]{0:T(128)S(1)}, f32[16]{0:T(128)}, u32[]{:S(2)}) copy-start(f32[16]{0:T(128)} %param.11) | copy-start | bytes 196
  27.5 0.7 %copy-start.7 = (f32[16]{0:T(128)S(1)}, f32[16]{0:T(128)}, u32[]{:S(2)}) copy-start(f32[16]{0:T(128)} %param.13) | copy-start | bytes 196
  29.5 5.5 %collective-permute-start.7 = (bf16[10,3,8,128]{3,2,1,0:T(8,128)(2,1)S(1)}, bf16[10,3,8,128]{3,2,1,0:T(8,128)(2,1)S(1)}, u32[]{:S(2)}, u32[]{:S(2)}) collective-permute-start(bf16[10,3,8,128]{3,2,1,0:T(8,128)(2,1)S(1)} %get-tuple-element.11), channel_id=1, source_target_pairs={{0,1},{1,2},{2,3},{3,4},{4,5},{5,6},{6,7},{7,0},{8,9},{9,10},{10,1... | collective-permute-start | bytes 184328 | tf_op jit(solution)/shard_map/ppermute | solution.py:32
  29.6 5.4 %collective-permute-start.8 = (bf16[10,3,8,128]{3,2,1,0:T(8,128)(2,1)S(1)}, bf16[10,3,8,128]{3,2,1,0:T(8,128)(2,1)S(1)}, u32[]{:S(2)}, u32[]{:S(2)}) collective-permute-start(bf16[10,3,8,128]{3,2,1,0:T(8,128)(2,1)S(1)} %get-tuple-element.12), channel_id=1, source_target_pairs={{1,0},{2,1},{3,2},{4,3},{5,4},{6,5},{7,6},{0,7},{9,8},{10,9},{11,1... | collective-permute-start | bytes 184328 | tf_op jit(solution)/shard_map/ppermute | solution.py:33
where the time goes:
time: 51.4 us; the launch traced here: 51 us
  Pallas kernels  18.1 us (35%)
  starting transfers between devices  15.6 us (30%)
  local copies, waits for them, and re-layouts  7.28 us (14%)
  other arithmetic  5.1 us (10%)
  waiting for transfers between devices  4.16 us (8%)
  between operations  0.74 us (1%)
    pallas_call x1, Pallas kernels, one_pair(): pl.pallas_call(partial(layers_kernel, tgt_cols=tgt_cols, inner=inner, cha...  13.6 us
    ppermute x5, starting transfers between devices, xor_blocks(): blocks = jnp.concatenate([blocks, lax.ppermute(blocks, axis, swap)], axis=0)  9.1 us
    ppermute x2, starting transfers between devices, cyclic_halo(): lax.ppermute(lax.slice_in_dim(block, 0, width, axis=dim), axis, backward)  4.97 us
    concatenate x5, other arithmetic, xor_blocks(): blocks = jnp.concatenate([blocks, lax.ppermute(blocks, axis, swap)], axis=0)  3.15 us
    ppermute x5, waiting for transfers between devices, xor_blocks(): blocks = jnp.concatenate([blocks, lax.ppermute(blocks, axis, swap)], axis=0)  2.9 us
    pallas_call x1, Pallas kernels, one_pair(): pl.pallas_call(partial(volume_kernel, src_cols=src_cols, tgt_cols=tgt_col...  2.26 us
    pallas_call x1, Pallas kernels, one_pair(): pl.pallas_call(partial(weights_kernel, inner=inner, rows_a=rows_a, rows_b...  2.19 us
    ppermute x2, starting transfers between devices, cyclic_halo(): lax.ppermute(lax.slice_in_dim(block, size - width, size, axis=dim), axis,...  1.55 us
  transfers between devices with their start and end apart: 9, of which 3 were waited for; matrix products, arithmetic and copies ran while one was open for 14% of the time, Pallas kernels for 4%

commit v1 on v0

--- a/solution.py
+++ b/solution.py
@@ -15,56 +15,68 @@
 
 def xor_blocks(block, axis):
     count = lax.axis_size(axis)
-    blocks = block[None]
-    step = 1
-    while step < count:
+    held, masks = block[None], [0]
+    pieces, piece_masks = [held], [[0]]
+    step = count // 2
+    while step:
         swap = [(i, i ^ step) for i in range(count)]
-        blocks = jnp.concatenate([blocks, lax.ppermute(blocks, axis, swap)], axis=0)
-        step *= 2
-    return blocks
-
-
-def cyclic_halo(block, axis, dim, width):
+        got = lax.ppermute(held, axis, swap)
+        got_masks = [m ^ step for m in masks]
+        pieces.append(got)
+        piece_masks.append(got_masks)
+        masks = masks + got_masks
+        if step > 1:
+            held = jnp.concatenate([held, got], axis=0)
+        step //= 2
+    return pieces, piece_masks
+
+
+def swap_edges(low_edge, high_edge, axis):
     count = lax.axis_size(axis)
-    size = block.shape[dim]
     forward = [(i, (i + 1) % count) for i in range(count)]
     backward = [((i + 1) % count, i) for i in range(count)]
-    low = lax.ppermute(lax.slice_in_dim(block, size - width, size, axis=dim), axis, forward)
-    high = lax.ppermute(lax.slice_in_dim(block, 0, width, axis=dim), axis, backward)
-    return jnp.concatenate([low, block, high], axis=dim)
-
-
-def wide_blocks(blocks, axis):
-    count, rows, chunk = blocks.shape
+    return lax.ppermute(high_edge, axis, forward), lax.ppermute(low_edge, axis, backward)
+
+
+def wide_blocks(pieces, masks, axis):
+    chunk = pieces[0].shape[-1]
     if chunk % LANES == 0:
-        return blocks, lax.axis_index(axis)
-    order = lax.axis_index(axis) ^ jnp.arange(count)
-    joined = jnp.take(blocks, order, axis=0).transpose(1, 0, 2).reshape(1, rows, count * chunk)
-    return joined, jnp.int32(0)
-
-
-def volume_kernel(pos_ref, src_ref, tgt_ref, out_ref, left_s, right_s, *, src_cols, tgt_cols):
-    def normed(blocks_ref, held, index):
-        count = blocks_ref.shape[0]
+        return pieces, masks, axis
+    flat = [m for group in masks for m in group]
+    blocks = jnp.concatenate(pieces, axis=0)
+    place = [flat.index(m) for m in range(len(flat))]
+    order = jnp.asarray(place, jnp.int32)[lax.axis_index(axis) ^ jnp.arange(len(flat))]
+    joined = jnp.take(blocks, order, axis=0).transpose(1, 0, 2)
+    return [joined.reshape(1, joined.shape[0], -1)], [[0]], None
+
+
+def volume_kernel(*refs, masks, axes, src_cols, tgt_cols):
+    counts = [len(group) for group in masks]
+    left_refs, right_refs = refs[: counts[0]], refs[counts[0] : sum(counts)]
+    out_ref, low_ref, high_ref, left_s, right_s = refs[sum(counts) :]
+
+    def normed(block_refs, block_masks, axis, held):
+        where = [(ref, n, m) for ref, group in zip(block_refs, block_masks) for n, m in enumerate(group)]
         squares = None
-        for m in range(count):
-            values = blocks_ref[m].astype(jnp.float32)
+        for ref, n, _ in where:
+            values = ref[n].astype(jnp.float32)
             part = jnp.sum(values * values, axis=-1, keepdims=True)
             squares = part if squares is None else squares + part
         scale = lax.rsqrt(squares + epsilon)
-        for m in range(count):
-            values = blocks_ref[m].astype(jnp.float32)
-            held[index ^ m] = (values * scale).astype(jnp.bfloat16)
-        return jnp.concatenate([held[m] for m in range(count)], axis=1)
-
-    left = normed(src_ref, left_s, pos_ref[0])
-    right = normed(tgt_ref, right_s, pos_ref[1])
+        index = 0 if axis is None else lax.axis_index(axis)
+        for ref, n, m in where:
+            held[index ^ m] = (ref[n].astype(jnp.float32) * scale).astype(jnp.bfloat16)
+        return jnp.concatenate([held[n] for n in range(len(where))], axis=1)
+
+    left = normed(left_refs, masks[0], axes[0], left_s)
+    right = normed(right_refs, masks[1], axes[1], right_s)
     volume = lax.dot_general(
         left, right, (((1,), (1,)), ((), ())), preferred_element_type=jnp.float32
     )
     blocks = LANES // tgt_cols
     inner = src_cols // blocks
-    for i in range(out_ref.shape[0]):
+    rows_a = out_ref.shape[0]
+    for i in range(rows_a):
         for k in range(out_ref.shape[1]):
             pieces = [
                 volume[
@@ -73,7 +85,12 @@
                 ]
                 for b in range(blocks)
             ]
-            out_ref[i, k] = jnp.concatenate(pieces, axis=1).astype(jnp.bfloat16)
+            plane = jnp.concatenate(pieces, axis=1).astype(jnp.bfloat16)
+            out_ref[i, k] = plane
+            if i < HALO:
+                low_ref[i, k] = plane
+            if i >= rows_a - HALO:
+                high_ref[i - rows_a + HALO, k] = plane
 
 
 def weights_kernel(one_ref, two_ref, three_ref, w1_ref, w2_ref, w3_ref, w3_s, *, inner, rows_a, rows_b):
@@ -145,12 +162,32 @@
 
 
 def layers_kernel(
-    pos_ref, b3_ref, vol_ref, w1_ref, w2_ref, w3_ref, b1_ref, b2_ref, out_ref, vj, a1, a2,
-    *, tgt_cols, inner, channels,
+    b1_ref, b2_ref, b3_ref, own_ref, low_a_ref, high_a_ref, low_b_ref, high_b_ref,
+    w1_ref, w2_ref, w3_ref, out_ref, vj, a1, a2, *, sizes, tgt_cols, inner, channels,
 ):
-    ext_a, ext_b = vol_ref.shape[0], vol_ref.shape[1]
-    first_a, count_a, first_b, count_b = pos_ref[0], pos_ref[1], pos_ref[2], pos_ref[3]
-    wide = inner * LANES
+    rows_a, rows_b = own_ref.shape[0], own_ref.shape[1]
+    ext_a, ext_b = rows_a + 2 * HALO, rows_b + 2 * HALO
+    count_a, count_b = sizes[0] * rows_a, sizes[1] * rows_b
+    first_a = lax.axis_index("src") * rows_a
+    first_b = lax.axis_index("tgt") * rows_b
+
+    def plane(a, b):
+        if b < HALO:
+            return low_b_ref[a, b]
+        if b >= HALO + rows_b:
+            return high_b_ref[a, b - HALO - rows_b]
+        if a < HALO:
+            return low_a_ref[a, b - HALO]
+        if a >= HALO + rows_a:
+            return high_a_ref[a - HALO - rows_a, b - HALO]
+        return own_ref[a - HALO, b - HALO]
+
+    def biases(ref):
+        row = lax.broadcasted_iota(jnp.int32, (channels, LANES), 0)
+        got = jnp.zeros((channels, LANES), jnp.float32)
+        for c in range(channels):
+            got = jnp.where(row == c, ref[c], got)
+        return got
 
     def inside(a, b, edge):
         ga = first_a + a - edge
@@ -170,9 +207,9 @@
 
     plane_row = lax.broadcasted_iota(jnp.int32, (inner, LANES), 0)
 
-    def spread_row(a, carry):
+    def spread_row(a):
         for b in range(ext_b):
-            x = vol_ref[a, b].astype(jnp.float32)
+            x = plane(a, b).astype(jnp.float32)
             x = jnp.where(inside(a, b, HALO), x, 0.0)
             before = up(x, tgt_cols, 0, LANES)
             after = down(x, tgt_cols, 0, LANES)
@@ -182,9 +219,9 @@
             vj[a, b, 0:rows] = up(both, 1, 0, tgt_cols).astype(jnp.bfloat16)
             vj[a, b, rows : 2 * rows] = both.astype(jnp.bfloat16)
             vj[a, b, 2 * rows : 3 * rows] = down(both, 1, 0, tgt_cols).astype(jnp.bfloat16)
-        return carry
-
-    lax.fori_loop(0, ext_a, spread_row, 0)
+
+    for a in range(ext_a):
+        spread_row(a)
 
     def put(dst, a, b, blocks):
         dst[a, b, 0:channels] = up(blocks[-1], tgt_cols, 0, LANES).astype(jnp.bfloat16)
@@ -193,11 +230,11 @@
         dst[a, b, (inner + 1) * channels :] = down(blocks[0], tgt_cols, 0, LANES).astype(jnp.bfloat16)
 
     l1_a, l1_b = ext_a - 2, ext_b - 2
-    bias1 = jnp.broadcast_to(b1_ref[...], (channels, LANES))
+    bias1 = biases(b1_ref)
     depth1 = TAPS * TAPS * TAPS * 2 * inner
     group = 4 if l1_b % 4 == 0 else 2
 
-    def first_row(a, carry):
+    def first_row(a):
         for b0 in range(0, l1_b, group):
             x = jnp.concatenate(
                 [
@@ -224,12 +261,12 @@
                     for c in range(inner)
                 ]
                 put(a1, a, b0 + n, blocks)
-        return carry
-
-    lax.fori_loop(0, l1_a, first_row, 0)
+
+    for a in range(l1_a):
+        first_row(a)
 
     l2_a, l2_b = l1_a - 2, l1_b - 2
-    bias2 = jnp.broadcast_to(b2_ref[...], (channels, LANES))
+    bias2 = biases(b2_ref)
     cells = 4 * channels
     half = inner // 2
 
@@ -237,9 +274,7 @@
         for b in range(l2_b, a2.shape[1]):
             a2[a, b] = jnp.zeros(a2.shape[2:], jnp.bfloat16)
 
-    def second_patch(n, carry):
-        pa = (n // (l2_b // 2)) * 2
-        pb = (n % (l2_b // 2)) * 2
+    def second_patch(pa, pb):
         for h in range(2):
             x = jnp.concatenate(
                 [
@@ -281,11 +316,13 @@
                             a2[pa + oi, pb + ok, (inner + 1) * channels :] = down(
                                 block, tgt_cols, 0, LANES
                             ).astype(jnp.bfloat16)
-        return carry
-
-    lax.fori_loop(0, (l2_a // 2) * (l2_b // 2), second_patch, 0)
-
-    cells = out_ref.shape[0]
+
+    for pa in range(0, l2_a, 2):
+        for pb in range(0, l2_b, 2):
+            second_patch(pa, pb)
+
+    cells = rows_a * rows_b
+    columns = []
     for h in range(2):
         x = jnp.concatenate(
             [
@@ -310,10 +347,13 @@
                 + up(part[:cells], 1, 0, tgt_cols)
                 + down(part[2 * cells :], 1, 0, tgt_cols)
             )
-            c = h * half + q
-            out_ref[:, c * LANES : (c + 1) * LANES] = jnp.maximum(total + b3_ref[0], 0.0).astype(
-                jnp.bfloat16
-            )
+            columns.append(jnp.maximum(total + b3_ref[0], 0.0))
+    scores = jnp.stack(columns, axis=0).swapaxes(0, 1)
+    for n in range(cells):
+        for b in range(LANES // tgt_cols):
+            out_ref[n // rows_b, n % rows_b, b * inner : (b + 1) * inner] = scores[
+                n, :, b * tgt_cols : (b + 1) * tgt_cols
+            ].astype(jnp.bfloat16)
 
 
 VMEM = pl.BlockSpec(memory_space=pltpu.VMEM)
@@ -329,10 +369,10 @@
     assert 2 * inner == channels and LANES % tgt_cols == 0
     assert rows_a % 2 == 0 and rows_b % 2 == 0 and min(rows_a, rows_b) >= HALO
 
-    left = xor_blocks(source.reshape(rows_a * src_cols, -1), "tgt")
-    right = xor_blocks(target.reshape(rows_b * tgt_cols, -1), "src")
-    left, left_at = wide_blocks(left, "tgt")
-    right, right_at = wide_blocks(right, "src")
+    left, left_masks = xor_blocks(source.reshape(rows_a * src_cols, -1), "tgt")
+    right, right_masks = xor_blocks(target.reshape(rows_b * tgt_cols, -1), "src")
+    left, left_masks, left_axis = wide_blocks(left, left_masks, "tgt")
+    right, right_masks, right_axis = wide_blocks(right, right_masks, "src")
 
     taps = TAPS**4
     w3_cols = TAPS * (rows_a + 2) * LANES
@@ -348,6 +388,7 @@
         out_specs=(VMEM, VMEM, VMEM),
         scratch_shapes=[pltpu.VMEM((TAPS * rows_a * rows_b, w3_cols), jnp.float32)],
         cost_estimate=pl.CostEstimate(flops=2_000_000_000, bytes_accessed=1_000_000, transcendentals=0),
+        compiler_params=pltpu.CompilerParams(vmem_limit_bytes=8 << 20),
         name="weights",
     )(
         conv_one.reshape(taps, channels),
@@ -355,41 +396,51 @@
         conv_three.reshape(taps, channels),
     )
 
-    volume = pl.pallas_call(
-        partial(volume_kernel, src_cols=src_cols, tgt_cols=tgt_cols),
-        out_shape=jax.ShapeDtypeStruct((rows_a, rows_b, inner, LANES), jnp.bfloat16),
-        in_specs=[SMEM, VMEM, VMEM],
-        out_specs=VMEM,
-        scratch_shapes=[pltpu.VMEM(left.shape, jnp.bfloat16), pltpu.VMEM(right.shape, jnp.bfloat16)],
+    def held(pieces):
+        return pltpu.VMEM((sum(p.shape[0] for p in pieces), *pieces[0].shape[1:]), jnp.bfloat16)
+
+    edge = jax.ShapeDtypeStruct((HALO, rows_b, inner, LANES), jnp.bfloat16)
+    own, low_edge, high_edge = pl.pallas_call(
+        partial(
+            volume_kernel,
+            masks=(left_masks, right_masks),
+            axes=(left_axis, right_axis),
+            src_cols=src_cols,
+            tgt_cols=tgt_cols,
+        ),
+        out_shape=(jax.ShapeDtypeStruct((rows_a, rows_b, inner, LANES), jnp.bfloat16), edge, edge),
+        in_specs=[VMEM] * (len(left) + len(right)),
+        out_specs=(VMEM,) * 3,
+        scratch_shapes=[held(left), held(right)],
+        compiler_params=pltpu.CompilerParams(vmem_limit_bytes=8 << 20),
         name="volume",
-    )(jnp.stack([left_at, right_at]).astype(jnp.int32), left, right)
-
-    volume = cyclic_halo(volume, "src", 0, HALO)
-    volume = cyclic_halo(volume, "tgt", 1, HALO)
+    )(*left, *right)
+
+    low_a, high_a = swap_edges(low_edge, high_edge, "src")
+    tall = [low_a, own, high_a]
+    low_edge = jnp.concatenate([x[:, :HALO] for x in tall], axis=0)
+    high_edge = jnp.concatenate([x[:, rows_b - HALO :] for x in tall], axis=0)
+    low_b, high_b = swap_edges(low_edge, high_edge, "tgt")
     ext_a, ext_b = rows_a + 2 * HALO, rows_b + 2 * HALO
-    place = jnp.stack(
-        [
-            lax.axis_index("src") * rows_a,
-            lax.axis_size("src") * rows_a,
-            lax.axis_index("tgt") * rows_b,
-            lax.axis_size("tgt") * rows_b,
-        ]
-    ).astype(jnp.int32)
-    wide_b = LANES // channels
-    scores = pl.pallas_call(
-        partial(layers_kernel, tgt_cols=tgt_cols, inner=inner, channels=channels),
-        out_shape=jax.ShapeDtypeStruct((rows_a * rows_b, inner * LANES), jnp.bfloat16),
-        in_specs=[SMEM, SMEM] + [VMEM] * 6,
+    return pl.pallas_call(
+        partial(
+            layers_kernel,
+            sizes=(lax.axis_size("src"), lax.axis_size("tgt")),
+            tgt_cols=tgt_cols,
+            inner=inner,
+            channels=channels,
+        ),
+        out_shape=jax.ShapeDtypeStruct((rows_a, rows_b, src_cols, tgt_cols), jnp.bfloat16),
+        in_specs=[SMEM] * 3 + [VMEM] * 8,
         out_specs=VMEM,
         scratch_shapes=[
             pltpu.VMEM((ext_a, ext_b, TAPS * 2 * inner, LANES), jnp.bfloat16),
             pltpu.VMEM((ext_a - 2, ext_b - 2, (inner + 2) * channels, LANES), jnp.bfloat16),
-            pltpu.VMEM((ext_a - 4, wide_b, (inner + 2) * channels, LANES), jnp.bfloat16),
+            pltpu.VMEM((ext_a - 4, LANES // channels, (inner + 2) * channels, LANES), jnp.bfloat16),
         ],
+        compiler_params=pltpu.CompilerParams(vmem_limit_bytes=20 << 20),
         name="layers",
-    )(place, bias_three, volume, w1, w2, w3, bias_one[:, None], bias_two[:, None])
-    scores = scores.reshape(rows_a, rows_b, inner, blocks, tgt_cols).transpose(0, 1, 3, 2, 4)
-    return scores.reshape(rows_a, rows_b, src_cols, tgt_cols)
+    )(bias_one, bias_two, bias_three, own, low_a, high_a, low_b, high_b, w1, w2, w3)
 
 
 def local(source_feats, target_feats, *params):

time: 51.4 us -> 35.8 us (0.70)
  Pallas kernels: 18.1 us -> 8.17 us
  waiting for transfers between devices: 4.16 us -> 9.54 us
  local copies, waits for them, and re-layouts: 7.28 us -> 2.21 us
  other arithmetic: 5.1 us -> 0.82 us
  starting transfers between devices: 15.6 us -> 14 us
    pallas_call x2, Pallas kernels: 15.9 us -> 7.78 us  [the longest x1 7.17 us: one_pair(): pl.pallas_call(partial(layers_kernel, sizes=(lax.axis_size('src'), lax.ax...]
    ppermute x9, waiting for transfers between devices: 4.16 us -> 9.54 us  [the longest x2 5.43 us: swap_edges(): lax.ppermute(high_edge, axis, forward)]
    concatenate x7 -> x5, other arithmetic: 3.87 us -> 0.82 us  [the longest x3 0.79 us: xor_blocks(): held = jnp.concatenate([held, got], axis=0)]
    pallas_call x1, Pallas kernels: 2.19 us -> 0.39 us  [one_pair(): pl.pallas_call(partial(weights_kernel, inner=inner, rows_a=rows_a, rows_b...]
    ppermute x9, starting transfers between devices: 15.6 us -> 14 us  [the longest x5 8.84 us: xor_blocks(): got = lax.ppermute(held, axis, swap)]
    broadcast_in_dim x2 -> x0, local copies, waits for them, and re-layouts: 1.35 us -> none  [the longest x1 0.68 us: one_pair(): bias_two[:, None]]
    another operation x2 -> x0, other arithmetic: 1.24 us -> none  [the longest x1 0.65 us: one_pair(): jnp.stack([lax.axis_index('src') * rows_a, lax.axis_size('src') * rows_a,...]
    reshape x1 -> x0, local copies, waits for them, and re-layouts: 0.92 us -> none  [one_pair(): scores.reshape(rows_a, rows_b, inner, blocks, tgt_cols)]
  transfers between devices with their start and end apart: 9 -> 9, of which waited for: 3 -> 7; matrix products, arithmetic and copies ran while one was open for 14% -> 3% of each run, Pallas kernels for 4% -> 1%
where the time goes in v1:
time: 35.8 us; the launch traced here: 35.5 us
  starting transfers between devices  14 us (39%)
  waiting for transfers between devices  9.54 us (27%)
  Pallas kernels  8.17 us (23%)
  local copies, waits for them, and re-layouts  2.21 us (6%)
  other arithmetic  0.82 us (2%)
  between operations  0.75 us (2%)
    ppermute x5, starting transfers between devices, xor_blocks(): got = lax.ppermute(held, axis, swap)  8.84 us
    pallas_call x1, Pallas kernels, one_pair(): pl.pallas_call(partial(layers_kernel, sizes=(lax.axis_size('src'), lax.ax...  7.17 us
    ppermute x2, waiting for transfers between devices, swap_edges(): lax.ppermute(high_edge, axis, forward)  5.43 us
    ppermute x2, starting transfers between devices, swap_edges(): lax.ppermute(low_edge, axis, backward)  3.6 us
    ppermute x5, waiting for transfers between devices, xor_blocks(): got = lax.ppermute(held, axis, swap)  2.78 us
    unnamed x14, local copies, waits for them, and re-layouts  1.94 us
    ppermute x2, starting transfers between devices, swap_edges(): lax.ppermute(high_edge, axis, forward)  1.61 us
    ppermute x2, waiting for transfers between devices, swap_edges(): lax.ppermute(low_edge, axis, backward)  1.33 us
  transfers between devices with their start and end apart: 9, of which 7 were waited for; matrix products, arithmetic and copies ran while one was open for 3% of the time, Pallas kernels for 1%

profile of v1, /device:TPU:0, one launch (start us, length us, event | category | flops | bytes accessed | tf_op | source)
XLA Modules:
  0.0 35.5 jit_solution(2392611974724539178)
XLA Ops:
  0.0 4.1 %collective-permute-start = (bf16[1,128,128]{2,1,0:T(8,128)(2,1)}, bf16[1,128,128]{2,1,0:T(8,128)(2,1)S(1)}, u32[]{:S(2)}, u32[]{:S(2)}) collective-permute-start(bf16[1,128,128]{2,1,0:T(8,128)(2,1)} %bitcast.12), channel_id=1, source_target_pairs={{0,4},{1,5},{2,6},{3,7},{4,0},{5,1},{6,2},{7,3},{8,12},{9,13},{10,... | collective-permute-start | bytes 98312 | tf_op jit(solution)/shard_map/ppermute | solution.py:23
  4.1 0.0 copy-start.1
  4.1 1.5 %collective-permute-start.3 = (bf16[1,128,256]{2,1,0:T(8,128)(2,1)}, bf16[1,128,256]{2,1,0:T(8,128)(2,1)S(1)}, u32[]{:S(2)}, u32[]{:S(2)}) collective-permute-start(bf16[1,128,256]{2,1,0:T(8,128)(2,1)} %bitcast.16), channel_id=1, source_target_pairs={{0,16},{8,24},{16,0},{24,8},{1,17},{9,25},{17,1},{25,9},{2,18},{10... | collective-permute-start | bytes 196616 | tf_op jit(solution)/shard_map/ppermute | solution.py:23
  5.6 0.9 %collective-permute-done.refs_1_ = bf16[1,128,128]{2,1,0:T(8,128)(2,1)S(1)} collective-permute-done((bf16[1,128,128]{2,1,0:T(8,128)(2,1)}, bf16[1,128,128]{2,1,0:T(8,128)(2,1)S(1)}, u32[]{:S(2)}, u32[]{:S(2)}) %collective-permute-start) | collective-permute-done | bytes 32800 | tf_op jit(solution)/shard_map/ppermute | solution.py:23
  6.5 0.8 %pad_maximum_fusion.2 = bf16[2,128,128]{2,1,0:T(8,128)(2,1)S(1)} fusion(bf16[1,128,128]{2,1,0:T(8,128)(2,1)S(1)} %collective-permute-done.refs_1_, bf16[1,128,128]{2,1,0:T(8,128)(2,1)} %bitcast.13), kind=kLoop, calls=%fused_computation.2 | loop fusion | flops 32768 | bytes 131072 | tf_op jit(solution)/shard_map/concatenate | solution.py:29
  7.3 0.0 copy-start
  7.3 0.0 copy-start.4
  7.3 1.6 %collective-permute-start.1 = (bf16[2,128,128]{2,1,0:T(8,128)(2,1)S(1)}, bf16[2,128,128]{2,1,0:T(8,128)(2,1)S(1)}, u32[]{:S(2)}, u32[]{:S(2)}) collective-permute-start(bf16[2,128,128]{2,1,0:T(8,128)(2,1)S(1)} %pad_maximum_fusion.2), channel_id=1, source_target_pairs={{0,2},{1,3},{2,0},{3,1},{4,6},{5,7},{6,4},{7,5},{8,10},{9,11},{10,... | collective-permute-start | bytes 196616 | tf_op jit(solution)/shard_map/ppermute | solution.py:23
  8.9 0.0 collective-permute-done.3.refs_5_
  8.9 0.0 copy-done.1
  8.9 1.6 %collective-permute-start.4 = (bf16[2,128,256]{2,1,0:T(8,128)(2,1)S(1)}, bf16[2,128,256]{2,1,0:T(8,128)(2,1)S(1)}, u32[]{:S(2)}, u32[]{:S(2)}) collective-permute-start(bf16[2,128,256]{2,1,0:T(8,128)(2,1)S(1)} %pad_maximum_fusion.1), channel_id=1, source_target_pairs={{0,8},{8,0},{16,24},{24,16},{1,9},{9,1},{17,25},{25,17},{2,10},{10... | collective-permute-start | bytes 393224 | tf_op jit(solution)/shard_map/ppermute | solution.py:23
  10.5 1.1 %collective-permute-done.1.refs_2_ = bf16[2,128,128]{2,1,0:T(8,128)(2,1)S(1)} collective-permute-done((bf16[2,128,128]{2,1,0:T(8,128)(2,1)S(1)}, bf16[2,128,128]{2,1,0:T(8,128)(2,1)S(1)}, u32[]{:S(2)}, u32[]{:S(2)}) %collective-permute-start.1) | collective-permute-done | bytes 65568 | tf_op jit(solution)/shard_map/ppermute | solution.py:23
  11.6 0.0 copy-done
  11.7 0.1 collective-permute-start.2
  11.7 0.0 copy-done.4
  11.7 0.0 copy-start.5
  11.8 0.2 copy.10
  12.0 0.5 %copy-done.5 = bf16[3,3,3,3,1,16]{5,3,4,2,1,0:T(4,128)(2,1)S(1)} copy-done((bf16[3,3,3,3,1,16]{5,3,4,2,1,0:T(4,128)(2,1)S(1)}, bf16[3,3,3,3,1,16]{5,3,4,2,1,0:T(4,128)(2,1)}, u32[]{:S(2)}) %copy-start.5) | copy-done | bytes 2616
  12.5 0.0 copy-start.6
  12.5 0.7 %copy-done.6 = bf16[3,3,3,3,16,1]{4,3,5,2,1,0:T(4,128)(2,1)S(1)} copy-done((bf16[3,3,3,3,16,1]{4,3,5,2,1,0:T(4,128)(2,1)S(1)}, bf16[3,3,3,3,16,1]{4,3,5,2,1,0:T(4,128)(2,1)}, u32[]{:S(2)}) %copy-start.6) | copy-done | bytes 2616
  13.3 0.7 %collective-permute-done.4.refs_6_ = bf16[2,128,256]{2,1,0:T(8,128)(2,1)S(1)} collective-permute-done((bf16[2,128,256]{2,1,0:T(8,128)(2,1)S(1)}, bf16[2,128,256]{2,1,0:T(8,128)(2,1)S(1)}, u32[]{:S(2)}, u32[]{:S(2)}) %collective-permute-start.4) | collective-permute-done | bytes 131104 | tf_op jit(solution)/shard_map/ppermute | solution.py:23
  14.0 0.0 collective-permute-done.2.refs_3_
  14.0 0.6 %volume.1 = (bf16[4,4,8,128]{3,2,1,0:T(8,128)(2,1)S(1)}, bf16[3,4,8,128]{3,2,1,0:T(8,128)(2,1)S(1)}, bf16[3,4,8,128]{3,2,1,0:T(8,128)(2,1)S(1)}) custom-call(bf16[1,128,128]{2,1,0:T(8,128)(2,1)S(1)} %bitcast.15, bf16[1,128,128]{2,1,0:T(8,128)(2,1)S(1)} %collective-permute-done.refs_1_, bf16[2,128,128]{2,1,0:T(8,128)(2,1)S(1)} %collective-permute-done.1.refs_2_, ...), custom_call_target="tpu_custom_call" | custom-call | tf_op jit(solution)/shard_map/volume/pallas_call | solution.py:403
  14.6 1.5 %collective-permute-start.5 = (bf16[3,4,8,128]{3,2,1,0:T(8,128)(2,1)S(1)}, bf16[3,4,8,128]{3,2,1,0:T(8,128)(2,1)S(1)}, u32[]{:S(2)}, u32[]{:S(2)}) collective-permute-start(bf16[3,4,8,128]{3,2,1,0:T(8,128)(2,1)S(1)} %get-tuple-element.12), channel_id=1, source_target_pairs={{0,8},{8,16},{16,24},{24,0},{1,9},{9,17},{17,25},{25,1},{2,10},{10... | collective-permute-start | bytes 73736 | tf_op jit(solution)/shard_map/ppermute | solution.py:38
  16.2 1.4 %collective-permute-start.6 = (bf16[3,4,8,128]{3,2,1,0:T(8,128)(2,1)S(1)}, bf16[3,4,8,128]{3,2,1,0:T(8,128)(2,1)S(1)}, u32[]{:S(2)}, u32[]{:S(2)}) collective-permute-start(bf16[3,4,8,128]{3,2,1,0:T(8,128)(2,1)S(1)} %get-tuple-element.13), channel_id=1, source_target_pairs={{8,0},{16,8},{24,16},{0,24},{9,1},{17,9},{25,17},{1,25},{10,2},{18... | collective-permute-start | bytes 73736 | tf_op jit(solution)/shard_map/ppermute | solution.py:38
  17.6 1.8 %collective-permute-done.5.low_a_ref = bf16[3,4,8,128]{3,2,1,0:T(8,128)(2,1)S(1)} collective-permute-done((bf16[3,4,8,128]{3,2,1,0:T(8,128)(2,1)S(1)}, bf16[3,4,8,128]{3,2,1,0:T(8,128)(2,1)S(1)}, u32[]{:S(2)}, u32[]{:S(2)}) %collective-permute-start.5) | collective-permute-done | bytes 24608 | tf_op jit(solution)/shard_map/ppermute | solution.py:38
  19.4 0.6 %collective-permute-done.6.high_a_ref = bf16[3,4,8,128]{3,2,1,0:T(8,128)(2,1)S(1)} collective-permute-done((bf16[3,4,8,128]{3,2,1,0:T(8,128)(2,1)S(1)}, bf16[3,4,8,128]{3,2,1,0:T(8,128)(2,1)S(1)}, u32[]{:S(2)}, u32[]{:S(2)}) %collective-permute-start.6) | collective-permute-done | bytes 24608 | tf_op jit(solution)/shard_map/ppermute | solution.py:38
  20.0 2.2 %collective-permute-start.8 = (bf16[10,3,8,128]{3,2,1,0:T(8,128)(2,1)S(1)}, bf16[10,3,8,128]{3,2,1,0:T(8,128)(2,1)S(1)}, u32[]{:S(2)}, u32[]{:S(2)}) collective-permute-start(bf16[10,3,8,128]{3,2,1,0:T(8,128)(2,1)S(1)} %pad_maximum_fusion.4), channel_id=1, source_target_pairs={{1,0},{2,1},{3,2},{4,3},{5,4},{6,5},{7,6},{0,7},{9,8},{10,9},{11,1... | collective-permute-start | bytes 184328 | tf_op jit(solution)/shard_map/ppermute | solution.py:38
  22.2 0.1 collective-permute-start.7
  22.3 0.4 %weights.1 = (bf16[128,512]{1,0:T(8,128)(2,1)S(1)}, bf16[192,768]{1,0:T(8,128)(2,1)S(1)}, bf16[48,2304]{1,0:T(8,128)(2,1)S(1)}) custom-call(bf16[81,16]{1,0:T(8,128)(2,1)S(1)} %reshape.12.one_ref, bf16[1296,16]{1,0:T(8,128)(2,1)S(1)} %bitcast.11, bf16[81,16]{1,0:T(8,128)(2,1)S(1)} %reshape.15.three_ref), custom_call_target="tpu_custom_call" | custom-call | flops 2000000000 | bytes 1000000 | tf_op jit(solution)/shard_map/weights/pallas_call | solution.py:380
  23.3 0.7 %collective-permute-done.8.high_b_ref = bf16[10,3,8,128]{3,2,1,0:T(8,128)(2,1)S(1)} collective-permute-done((bf16[10,3,8,128]{3,2,1,0:T(8,128)(2,1)S(1)}, bf16[10,3,8,128]{3,2,1,0:T(8,128)(2,1)S(1)}, u32[]{:S(2)}, u32[]{:S(2)}) %collective-permute-start.8) | collective-permute-done | bytes 61472 | tf_op jit(solution)/shard_map/ppermute | solution.py:38
  24.0 3.6 %collective-permute-done.7.low_b_ref = bf16[10,3,8,128]{3,2,1,0:T(8,128)(2,1)S(1)} collective-permute-done((bf16[10,3,8,128]{3,2,1,0:T(8,128)(2,1)S(1)}, bf16[10,3,8,128]{3,2,1,0:T(8,128)(2,1)S(1)}, u32[]{:S(2)}, u32[]{:S(2)}) %collective-permute-start.7) | collective-permute-done | bytes 61472 | tf_op jit(solution)/shard_map/ppermute | solution.py:38
  27.7 0.0 copy-start.2
  27.7 0.0 copy-start.3
  27.7 0.7 %copy-done.2 = f32[16]{0:T(128)S(1)} copy-done((f32[16]{0:T(128)S(1)}, f32[16]{0:T(128)}, u32[]{:S(2)}) %copy-start.2) | copy-done | bytes 88
  28.3 0.0 copy-done.3
  28.4 7.2 %layers.1 = bf16[4,4,32,32]{3,2,1,0:T(8,128)(2,1)} custom-call(f32[16]{0:T(128)S(1)} %copy-done.2, f32[16]{0:T(128)S(1)} %copy-done.3, f32[1]{0:T(128)S(6)} %copy.11.b3_ref, bf16[4,4,8,128]{3,2,1,0:T(8,128)(2,1)S(1)} %get-tuple-element.11.own_ref, bf16[3,4,8,128]{3,2,1,0:T(8,128)(2,1)S(1)} %collective-permute-done.5.low_a_ref, ...), custom_call_target="tpu_custom_call" | custom-call | tf_op jit(solution)/shard_map/layers/pallas_call | solution.py:425
  (9 shorter events, 0.1 us)
Async XLA Ops:
  0.0 6.5 %collective-permute-start = (bf16[1,128,128]{2,1,0:T(8,128)(2,1)}, bf16[1,128,128]{2,1,0:T(8,128)(2,1)S(1)}, u32[]{:S(2)}, u32[]{:S(2)}) collective-permute-start(bf16[1,128,128]{2,1,0:T(8,128)(2,1)} %bitcast.12), channel_id=1, source_target_pairs={{0,4},{1,5},{2,6},{3,7},{4,0},{5,1},{6,2},{7,3},{8,12},{9,13},{10,... | collective-permute-start | bytes 98312 | tf_op jit(solution)/shard_map/ppermute | solution.py:23
  4.1 4.9 %copy-start.1 = (bf16[1,4,32,256]{3,2,1,0:T(8,128)(2,1)S(1)}, bf16[1,4,32,256]{3,2,1,0:T(8,128)(2,1)}, u32[]{:S(2)}) copy-start(bf16[1,4,32,256]{3,2,1,0:T(8,128)(2,1)} %param.9) | copy-start | bytes 196612
  4.1 4.9 %collective-permute-start.3 = (bf16[1,128,256]{2,1,0:T(8,128)(2,1)}, bf16[1,128,256]{2,1,0:T(8,128)(2,1)S(1)}, u32[]{:S(2)}, u32[]{:S(2)}) collective-permute-start(bf16[1,128,256]{2,1,0:T(8,128)(2,1)} %bitcast.16), channel_id=1, source_target_pairs={{0,16},{8,24},{16,0},{24,8},{1,17},{9,25},{17,1},{25,9},{2,18},{10... | collective-permute-start | bytes 196616 | tf_op jit(solution)/shard_map/ppermute | solution.py:23
  7.3 4.4 %copy-start = (bf16[1,4,32,128]{3,2,1,0:T(8,128)(2,1)S(1)}, bf16[1,4,32,128]{3,2,1,0:T(8,128)(2,1)}, u32[]{:S(2)}) copy-start(bf16[1,4,32,128]{3,2,1,0:T(8,128)(2,1)} %param.8) | copy-start | bytes 98308
  7.3 4.4 %copy-start.4 = (bf16[3,3,3,3,16,16]{5,4,3,2,1,0:T(8,128)(2,1)S(1)}, bf16[3,3,3,3,16,16]{5,4,3,2,1,0:T(8,128)(2,1)}, u32[]{:S(2)}) copy-start(bf16[3,3,3,3,16,16]{5,4,3,2,1,0:T(8,128)(2,1)} %param.12) | copy-start | bytes 124420
  7.3 4.3 %collective-permute-start.1 = (bf16[2,128,128]{2,1,0:T(8,128)(2,1)S(1)}, bf16[2,128,128]{2,1,0:T(8,128)(2,1)S(1)}, u32[]{:S(2)}, u32[]{:S(2)}) collective-permute-start(bf16[2,128,128]{2,1,0:T(8,128)(2,1)S(1)} %pad_maximum_fusion.2), channel_id=1, source_target_pairs={{0,2},{1,3},{2,0},{3,1},{4,6},{5,7},{6,4},{7,5},{8,10},{9,11},{10,... | collective-permute-start | bytes 196616 | tf_op jit(solution)/shard_map/ppermute | solution.py:23
  8.9 5.0 %collective-permute-start.4 = (bf16[2,128,256]{2,1,0:T(8,128)(2,1)S(1)}, bf16[2,128,256]{2,1,0:T(8,128)(2,1)S(1)}, u32[]{:S(2)}, u32[]{:S(2)}) collective-permute-start(bf16[2,128,256]{2,1,0:T(8,128)(2,1)S(1)} %pad_maximum_fusion.1), channel_id=1, source_target_pairs={{0,8},{8,0},{16,24},{24,16},{1,9},{9,1},{17,25},{25,17},{2,10},{10... | collective-permute-start | bytes 393224 | tf_op jit(solution)/shard_map/ppermute | solution.py:23
  11.7 2.3 %collective-permute-start.2 = (bf16[4,128,128]{2,1,0:T(8,128)(2,1)S(1)}, bf16[4,128,128]{2,1,0:T(8,128)(2,1)S(1)}, u32[]{:S(2)}, u32[]{:S(2)}) collective-permute-start(bf16[4,128,128]{2,1,0:T(8,128)(2,1)S(1)} %pad_maximum_fusion), channel_id=1, source_target_pairs={{0,1},{1,0},{2,3},{3,2},{4,5},{5,4},{6,7},{7,6},{8,9},{9,8},{10,11... | collective-permute-start | bytes 393224 | tf_op jit(solution)/shard_map/ppermute | solution.py:23
  11.7 0.7 %copy-start.5 = (bf16[3,3,3,3,1,16]{5,3,4,2,1,0:T(4,128)(2,1)S(1)}, bf16[3,3,3,3,1,16]{5,3,4,2,1,0:T(4,128)(2,1)}, u32[]{:S(2)}) copy-start(bf16[3,3,3,3,1,16]{5,3,4,2,1,0:T(4,128)(2,1)} %param.10) | copy-start | bytes 7780
  12.5 0.7 %copy-start.6 = (bf16[3,3,3,3,16,1]{4,3,5,2,1,0:T(4,128)(2,1)S(1)}, bf16[3,3,3,3,16,1]{4,3,5,2,1,0:T(4,128)(2,1)}, u32[]{:S(2)}) copy-start(bf16[3,3,3,3,16,1]{4,3,5,2,1,0:T(4,128)(2,1)} %param.14) | copy-start | bytes 7780
  14.6 4.8 %collective-permute-start.5 = (bf16[3,4,8,128]{3,2,1,0:T(8,128)(2,1)S(1)}, bf16[3,4,8,128]{3,2,1,0:T(8,128)(2,1)S(1)}, u32[]{:S(2)}, u32[]{:S(2)}) collective-permute-start(bf16[3,4,8,128]{3,2,1,0:T(8,128)(2,1)S(1)} %get-tuple-element.12), channel_id=1, source_target_pairs={{0,8},{8,16},{16,24},{24,0},{1,9},{9,17},{17,25},{25,1},{2,10},{10... | collective-permute-start | bytes 73736 | tf_op jit(solution)/shard_map/ppermute | solution.py:38
  16.2 3.8 %collective-permute-start.6 = (bf16[3,4,8,128]{3,2,1,0:T(8,128)(2,1)S(1)}, bf16[3,4,8,128]{3,2,1,0:T(8,128)(2,1)S(1)}, u32[]{:S(2)}, u32[]{:S(2)}) collective-permute-start(bf16[3,4,8,128]{3,2,1,0:T(8,128)(2,1)S(1)} %get-tuple-element.13), channel_id=1, source_target_pairs={{8,0},{16,8},{24,16},{0,24},{9,1},{17,9},{25,17},{1,25},{10,2},{18... | collective-permute-start | bytes 73736 | tf_op jit(solution)/shard_map/ppermute | solution.py:38
  20.0 4.0 %collective-permute-start.8 = (bf16[10,3,8,128]{3,2,1,0:T(8,128)(2,1)S(1)}, bf16[10,3,8,128]{3,2,1,0:T(8,128)(2,1)S(1)}, u32[]{:S(2)}, u32[]{:S(2)}) collective-permute-start(bf16[10,3,8,128]{3,2,1,0:T(8,128)(2,1)S(1)} %pad_maximum_fusion.4), channel_id=1, source_target_pairs={{1,0},{2,1},{3,2},{4,3},{5,4},{6,5},{7,6},{0,7},{9,8},{10,9},{11,1... | collective-permute-start | bytes 184328 | tf_op jit(solution)/shard_map/ppermute | solution.py:38
  22.2 5.5 %collective-permute-start.7 = (bf16[10,3,8,128]{3,2,1,0:T(8,128)(2,1)S(1)}, bf16[10,3,8,128]{3,2,1,0:T(8,128)(2,1)S(1)}, u32[]{:S(2)}, u32[]{:S(2)}) collective-permute-start(bf16[10,3,8,128]{3,2,1,0:T(8,128)(2,1)S(1)} %pad_maximum_fusion.3), channel_id=1, source_target_pairs={{0,1},{1,2},{2,3},{3,4},{4,5},{5,6},{6,7},{7,0},{8,9},{9,10},{10,1... | collective-permute-start | bytes 184328 | tf_op jit(solution)/shard_map/ppermute | solution.py:38
  27.7 0.7 %copy-start.2 = (f32[16]{0:T(128)S(1)}, f32[16]{0:T(128)}, u32[]{:S(2)}) copy-start(f32[16]{0:T(128)} %b1_ref.1) | copy-start | bytes 196
  27.7 0.7 %copy-start.3 = (f32[16]{0:T(128)S(1)}, f32[16]{0:T(128)}, u32[]{:S(2)}) copy-start(f32[16]{0:T(128)} %b2_ref.1) | copy-start | bytes 196

commit v2 on v1

--- a/solution.py
+++ b/solution.py
@@ -93,21 +93,30 @@
                 high_ref[i - rows_a + HALO, k] = plane
 
 
-def weights_kernel(one_ref, two_ref, three_ref, w1_ref, w2_ref, w3_ref, w3_s, *, inner, rows_a, rows_b):
-    channels = one_ref.shape[1]
+def weights_kernel(
+    b1_ref, b2_ref, b3_ref, one_ref, two_ref, three_ref, bias_ref, w1_ref, w2_ref, w3_ref, w3_s,
+    *, inner, rows_a, rows_b,
+):
+    channels = one_ref.shape[2]
     per_row = LANES // channels
     lane = lax.broadcasted_iota(jnp.int32, (channels, LANES), 1)
     row = lax.broadcasted_iota(jnp.int32, (channels, LANES), 0)
     lane_block = lane // channels
     spread = (lane % channels == row).astype(jnp.bfloat16)
 
-    def tiled(ref):
-        return jnp.dot(ref[...], spread, preferred_element_type=jnp.float32)
+    def tiled(values):
+        return jnp.dot(values, spread, preferred_element_type=jnp.float32)
+
+    for n, ref in enumerate((b1_ref, b2_ref, b3_ref)):
+        plane = jnp.zeros((channels, LANES), jnp.float32)
+        for c in range(channels):
+            plane = jnp.where(row == c, ref[c if n < 2 else 0], plane)
+        bias_ref[n] = plane
 
     def tap(a, b, e, g):
         return ((a * TAPS + b) * TAPS + e) * TAPS + g
 
-    one = tiled(one_ref)
+    one = [tiled(one_ref[:, g, :]) for g in range(TAPS)]
     column = jnp.where(row < inner, row, jnp.where(row == inner, inner, -2))
     column = jnp.where(row == 2 * inner - 1, -1, column)
     slabs = []
@@ -116,15 +125,15 @@
             for g in range(TAPS):
                 slab = jnp.zeros((channels, LANES), jnp.float32)
                 for b in range(TAPS):
-                    n = tap(a, b, e, g)
+                    n = tap(a, b, e, 0) // TAPS
                     hit = (column - lane_block == b - 1) & (column >= -1)
-                    slab = jnp.where(hit, one[n : n + 1], slab)
+                    slab = jnp.where(hit, one[g][n : n + 1], slab)
                 slabs.append(slab)
     while (len(slabs) * channels) % LANES:
         slabs.append(jnp.zeros((channels, LANES), jnp.float32))
     w1_ref[...] = jnp.concatenate(slabs, axis=0).T.astype(jnp.bfloat16)
 
-    two = tiled(two_ref)
+    two = tiled(two_ref[...])
     for b in range(TAPS):
         for half in range(2):
             col = (b * 2 + half) * LANES
@@ -143,7 +152,7 @@
                         at = ((g * 2 + oi) * 2 + ok) * channels
                         w2_ref[at : at + channels, col : col + LANES] = block.astype(jnp.bfloat16)
 
-    three = tiled(three_ref)
+    three = [tiled(three_ref[:, g, :]) for g in range(TAPS)]
     w3_s[...] = jnp.zeros_like(w3_s)
     lane_k = lax.broadcasted_iota(jnp.int32, (rows_b, LANES), 1) // channels
     row_k = lax.broadcasted_iota(jnp.int32, (rows_b, LANES), 0)
@@ -152,17 +161,17 @@
             for g in range(TAPS):
                 block = jnp.zeros((rows_b, LANES), jnp.float32)
                 for e in range(TAPS):
-                    n = tap(a, b, e, g)
-                    block = jnp.where(lane_k - row_k == e, three[n : n + 1], block)
+                    n = tap(a, b, e, 0) // TAPS
+                    block = jnp.where(lane_k - row_k == e, three[g][n : n + 1], block)
                 for oi in range(rows_a):
-                    col = (b * (rows_a + 2) + oi + a) * LANES
-                    at = (g * rows_a + oi) * rows_b
+                    col = (oi + a) * LANES
+                    at = ((g * TAPS + b) * rows_a + oi) * rows_b
                     w3_s[at : at + rows_b, col : col + LANES] = block
     w3_ref[...] = w3_s[...].astype(jnp.bfloat16)
 
 
 def layers_kernel(
-    b1_ref, b2_ref, b3_ref, own_ref, low_a_ref, high_a_ref, low_b_ref, high_b_ref,
+    bias_ref, own_ref, low_a_ref, high_a_ref, low_b_ref, high_b_ref,
     w1_ref, w2_ref, w3_ref, out_ref, vj, a1, a2, *, sizes, tgt_cols, inner, channels,
 ):
     rows_a, rows_b = own_ref.shape[0], own_ref.shape[1]
@@ -182,13 +191,6 @@
             return high_a_ref[a - HALO - rows_a, b - HALO]
         return own_ref[a - HALO, b - HALO]
 
-    def biases(ref):
-        row = lax.broadcasted_iota(jnp.int32, (channels, LANES), 0)
-        got = jnp.zeros((channels, LANES), jnp.float32)
-        for c in range(channels):
-            got = jnp.where(row == c, ref[c], got)
-        return got
-
     def inside(a, b, edge):
         ga = first_a + a - edge
         gb = first_b + b - edge
@@ -197,11 +199,11 @@
     def lanes(rows):
         return lax.broadcasted_iota(jnp.int32, (rows, LANES), 1)
 
-    def up(x, step, unit, size):
+    def up(x, step, size):
         pos = lanes(x.shape[0]) % size
         return jnp.where(pos >= step, pltpu.roll(x, step, 1), 0.0)
 
-    def down(x, step, unit, size):
+    def down(x, step, size):
         pos = lanes(x.shape[0]) % size
         return jnp.where(pos < size - step, pltpu.roll(x, LANES - step, 1), 0.0)
 
@@ -211,26 +213,26 @@
         for b in range(ext_b):
             x = plane(a, b).astype(jnp.float32)
             x = jnp.where(inside(a, b, HALO), x, 0.0)
-            before = up(x, tgt_cols, 0, LANES)
-            after = down(x, tgt_cols, 0, LANES)
+            before = up(x, tgt_cols, LANES)
+            after = down(x, tgt_cols, LANES)
             edge = jnp.where(plane_row == inner - 1, before, jnp.where(plane_row == 0, after, 0.0))
             both = jnp.concatenate([x, edge], axis=0)
             rows = 2 * inner
-            vj[a, b, 0:rows] = up(both, 1, 0, tgt_cols).astype(jnp.bfloat16)
+            vj[a, b, 0:rows] = up(both, 1, tgt_cols).astype(jnp.bfloat16)
             vj[a, b, rows : 2 * rows] = both.astype(jnp.bfloat16)
-            vj[a, b, 2 * rows : 3 * rows] = down(both, 1, 0, tgt_cols).astype(jnp.bfloat16)
+            vj[a, b, 2 * rows : 3 * rows] = down(both, 1, tgt_cols).astype(jnp.bfloat16)
 
     for a in range(ext_a):
         spread_row(a)
 
     def put(dst, a, b, blocks):
-        dst[a, b, 0:channels] = up(blocks[-1], tgt_cols, 0, LANES).astype(jnp.bfloat16)
+        dst[a, b, 0:channels] = up(blocks[-1], tgt_cols, LANES).astype(jnp.bfloat16)
         for n, block in enumerate(blocks):
             dst[a, b, (n + 1) * channels : (n + 2) * channels] = block.astype(jnp.bfloat16)
-        dst[a, b, (inner + 1) * channels :] = down(blocks[0], tgt_cols, 0, LANES).astype(jnp.bfloat16)
+        dst[a, b, (inner + 1) * channels :] = down(blocks[0], tgt_cols, LANES).astype(jnp.bfloat16)
 
     l1_a, l1_b = ext_a - 2, ext_b - 2
-    bias1 = biases(b1_ref)
+    bias1 = bias_ref[0]
     depth1 = TAPS * TAPS * TAPS * 2 * inner
     group = 4 if l1_b % 4 == 0 else 2
 
@@ -266,13 +268,9 @@
         first_row(a)
 
     l2_a, l2_b = l1_a - 2, l1_b - 2
-    bias2 = biases(b2_ref)
+    bias2 = bias_ref[1]
     cells = 4 * channels
     half = inner // 2
-
-    for a in range(l2_a):
-        for b in range(l2_b, a2.shape[1]):
-            a2[a, b] = jnp.zeros(a2.shape[2:], jnp.bfloat16)
 
     def second_patch(pa, pb):
         for h in range(2):
@@ -296,8 +294,8 @@
                 part = got[:, q * LANES : (q + 1) * LANES]
                 total = (
                     part[cells : 2 * cells]
-                    + up(part[:cells], 1, 0, tgt_cols)
-                    + down(part[2 * cells :], 1, 0, tgt_cols)
+                    + up(part[:cells], 1, tgt_cols)
+                    + down(part[2 * cells :], 1, tgt_cols)
                 )
                 c = h * half + q
                 for oi in range(2):
@@ -305,33 +303,25 @@
                         at = (oi * 2 + ok) * channels
                         block = jnp.maximum(total[at : at + channels] + bias2, 0.0)
                         block = jnp.where(inside(pa + oi, pb + ok, HALO - 2), block, 0.0)
-                        a2[pa + oi, pb + ok, (c + 1) * channels : (c + 2) * channels] = block.astype(
+                        a2[pa + oi, pb + ok, c * channels : (c + 1) * channels] = block.astype(
                             jnp.bfloat16
                         )
-                        if c == inner - 1:
-                            a2[pa + oi, pb + ok, 0:channels] = up(block, tgt_cols, 0, LANES).astype(
-                                jnp.bfloat16
-                            )
-                        if c == 0:
-                            a2[pa + oi, pb + ok, (inner + 1) * channels :] = down(
-                                block, tgt_cols, 0, LANES
-                            ).astype(jnp.bfloat16)
 
     for pa in range(0, l2_a, 2):
         for pb in range(0, l2_b, 2):
             second_patch(pa, pb)
 
     cells = rows_a * rows_b
-    columns = []
+    nothing = jnp.zeros((channels, LANES), jnp.bfloat16)
+    parts = []
     for h in range(2):
         x = jnp.concatenate(
             [
                 jnp.concatenate(
                     [
-                        a2[wi, wk, (c + dj) * channels : (c + dj + 1) * channels]
-                        for dj in range(TAPS)
+                        a2[wi, wk, c * channels : (c + 1) * channels] if wk < l2_b else nothing
                         for wi in range(l2_a)
-                        for wk in range(a2.shape[1])
+                        for wk in range(LANES // channels)
                     ],
                     axis=0,
                 )
@@ -340,14 +330,33 @@
             axis=1,
         )
         got = jnp.dot(w3_ref[...], x, preferred_element_type=jnp.float32)
-        for q in range(half):
-            part = got[:, q * LANES : (q + 1) * LANES]
-            total = (
-                part[cells : 2 * cells]
-                + up(part[:cells], 1, 0, tgt_cols)
-                + down(part[2 * cells :], 1, 0, tgt_cols)
-            )
-            columns.append(jnp.maximum(total + b3_ref[0], 0.0))
+        parts += [got[:, q * LANES : (q + 1) * LANES] for q in range(half)]
+
+    def column_sum(c, g):
+        total = None
+        for b in range(TAPS):
+            at = (g * TAPS + b) * cells
+            n = c + b - 1
+            if n < 0:
+                part = up(parts[-1][at : at + cells], tgt_cols, LANES)
+            elif n >= inner:
+                part = down(parts[0][at : at + cells], tgt_cols, LANES)
+            else:
+                part = parts[n][at : at + cells]
+            total = part if total is None else total + part
+        return total
+
+    bias3 = bias_ref[2]
+    columns = [
+        jnp.maximum(
+            column_sum(c, 1)
+            + up(column_sum(c, 0), 1, tgt_cols)
+            + down(column_sum(c, 2), 1, tgt_cols)
+            + bias3,
+            0.0,
+        )
+        for c in range(inner)
+    ]
     scores = jnp.stack(columns, axis=0).swapaxes(0, 1)
     for n in range(cells):
         for b in range(LANES // tgt_cols):
@@ -375,25 +384,30 @@
     right, right_masks, right_axis = wide_blocks(right, right_masks, "src")
 
     taps = TAPS**4
-    w3_cols = TAPS * (rows_a + 2) * LANES
+    w3_cols = (rows_a + 2) * LANES
+    w3_rows = TAPS * TAPS * rows_a * rows_b
     w1_cols = -(-(TAPS**3 * channels) // LANES) * LANES
-    w1, w2, w3 = pl.pallas_call(
+    biases, w1, w2, w3 = pl.pallas_call(
         partial(weights_kernel, inner=inner, rows_a=rows_a, rows_b=rows_b),
         out_shape=(
+            jax.ShapeDtypeStruct((TAPS, channels, LANES), jnp.float32),
             jax.ShapeDtypeStruct((LANES, w1_cols), jnp.bfloat16),
             jax.ShapeDtypeStruct((TAPS * 4 * channels, TAPS * 2 * LANES), jnp.bfloat16),
-            jax.ShapeDtypeStruct((TAPS * rows_a * rows_b, w3_cols), jnp.bfloat16),
+            jax.ShapeDtypeStruct((w3_rows, w3_cols), jnp.bfloat16),
         ),
-        in_specs=[VMEM] * 3,
-        out_specs=(VMEM, VMEM, VMEM),
-        scratch_shapes=[pltpu.VMEM((TAPS * rows_a * rows_b, w3_cols), jnp.float32)],
+        in_specs=[SMEM] * 3 + [VMEM] * 3,
+        out_specs=(VMEM,) * 4,
+        scratch_shapes=[pltpu.VMEM((w3_rows, w3_cols), jnp.float32)],
         cost_estimate=pl.CostEstimate(flops=2_000_000_000, bytes_accessed=1_000_000, transcendentals=0),
         compiler_params=pltpu.CompilerParams(vmem_limit_bytes=8 << 20),
         name="weights",
     )(
-        conv_one.reshape(taps, channels),
+        bias_one,
+        bias_two,
+        bias_three,
+        conv_one.reshape(-1, TAPS, channels),
         conv_two.reshape(taps, channels, channels).swapaxes(1, 2).reshape(taps * channels, channels),
-        conv_three.reshape(taps, channels),
+        conv_three.reshape(-1, TAPS, channels),
     )
 
     def held(pieces):
@@ -431,16 +445,16 @@
             channels=channels,
         ),
         out_shape=jax.ShapeDtypeStruct((rows_a, rows_b, src_cols, tgt_cols), jnp.bfloat16),
-        in_specs=[SMEM] * 3 + [VMEM] * 8,
+        in_specs=[VMEM] * 9,
         out_specs=VMEM,
         scratch_shapes=[
             pltpu.VMEM((ext_a, ext_b, TAPS * 2 * inner, LANES), jnp.bfloat16),
             pltpu.VMEM((ext_a - 2, ext_b - 2, (inner + 2) * channels, LANES), jnp.bfloat16),
-            pltpu.VMEM((ext_a - 4, LANES // channels, (inner + 2) * channels, LANES), jnp.bfloat16),
+            pltpu.VMEM((ext_a - 4, ext_b - 4, inner * channels, LANES), jnp.bfloat16),
         ],
         compiler_params=pltpu.CompilerParams(vmem_limit_bytes=20 << 20),
         name="layers",
-    )(bias_one, bias_two, bias_three, own, low_a, high_a, low_b, high_b, w1, w2, w3)
+    )(biases, own, low_a, high_a, low_b, high_b, w1, w2, w3)
 
 
 def local(source_feats, target_feats, *params):

time: 35.8 us -> 32 us (0.89)
  waiting for transfers between devices: 9.54 us -> 6.13 us
  starting transfers between devices: 14 us -> 15.4 us
  local copies, waits for them, and re-layouts: 2.21 us -> 0.91 us
  Pallas kernels: 8.17 us -> 7.76 us
    ppermute x2, waiting for transfers between devices: 5.43 us -> 0.29 us  [swap_edges(): lax.ppermute(high_edge, axis, forward)]
    ppermute x2, starting transfers between devices: 3.6 us -> 4.98 us  [swap_edges(): lax.ppermute(low_edge, axis, backward)]
    unnamed x14, local copies, waits for them, and re-layouts: 1.94 us -> 0.69 us
    ppermute x2, waiting for transfers between devices: 1.33 us -> 2.39 us  [swap_edges(): lax.ppermute(low_edge, axis, backward)]
    pallas_call x1, Pallas kernels: 7.17 us -> 6.18 us  [one_pair(): pl.pallas_call(partial(layers_kernel, sizes=(lax.axis_size('src'), lax.ax...]
    ppermute x5, waiting for transfers between devices: 2.78 us -> 3.45 us  [xor_blocks(): got = lax.ppermute(held, axis, swap)]
    pallas_call x1, Pallas kernels: 0.39 us -> 0.97 us  [one_pair(): pl.pallas_call(partial(weights_kernel, inner=inner, rows_a=rows_a, rows_b...]
  transfers between devices with their start and end apart: 9 -> 9, of which waited for: 7 -> 5; matrix products, arithmetic and copies ran while one was open for 3% -> 3% of each run, Pallas kernels for 1% -> 3%
where the time goes in v2:
time: 32 us; the launch traced here: 31.8 us
  starting transfers between devices  15.4 us (48%)
  Pallas kernels  7.76 us (24%)
  waiting for transfers between devices  6.13 us (19%)
  local copies, waits for them, and re-layouts  0.91 us (3%)
  other arithmetic  0.82 us (3%)
  between operations  0.77 us (2%)
    ppermute x5, starting transfers between devices, xor_blocks(): got = lax.ppermute(held, axis, swap)  8.84 us
    pallas_call x1, Pallas kernels, one_pair(): pl.pallas_call(partial(layers_kernel, sizes=(lax.axis_size('src'), lax.ax...  6.18 us
    ppermute x2, starting transfers between devices, swap_edges(): lax.ppermute(low_edge, axis, backward)  4.98 us
    ppermute x5, waiting for transfers between devices, xor_blocks(): got = lax.ppermute(held, axis, swap)  3.45 us
    ppermute x2, waiting for transfers between devices, swap_edges(): lax.ppermute(low_edge, axis, backward)  2.39 us
    ppermute x2, starting transfers between devices, swap_edges(): lax.ppermute(high_edge, axis, forward)  1.61 us
    pallas_call x1, Pallas kernels, one_pair(): pl.pallas_call(partial(weights_kernel, inner=inner, rows_a=rows_a, rows_b...  0.97 us
    concatenate x3, other arithmetic, xor_blocks(): held = jnp.concatenate([held, got], axis=0)  0.79 us
  transfers between devices with their start and end apart: 9, of which 5 were waited for; matrix products, arithmetic and copies ran while one was open for 3% of the time, Pallas kernels for 3%

profile of v2, /device:TPU:0, one launch (start us, length us, event | category | flops | bytes accessed | tf_op | source)
XLA Modules:
  0.0 31.8 jit_solution(3020150951284521686)
XLA Ops:
  0.0 4.1 %collective-permute-start = (bf16[1,128,128]{2,1,0:T(8,128)(2,1)}, bf16[1,128,128]{2,1,0:T(8,128)(2,1)S(1)}, u32[]{:S(2)}, u32[]{:S(2)}) collective-permute-start(bf16[1,128,128]{2,1,0:T(8,128)(2,1)} %bitcast.10), channel_id=1, source_target_pairs={{0,4},{1,5},{2,6},{3,7},{4,0},{5,1},{6,2},{7,3},{8,12},{9,13},{10,... | collective-permute-start | bytes 98312 | tf_op jit(solution)/shard_map/ppermute | solution.py:23
  4.1 0.0 copy-start.1
  4.1 1.5 %collective-permute-start.3 = (bf16[1,128,256]{2,1,0:T(8,128)(2,1)}, bf16[1,128,256]{2,1,0:T(8,128)(2,1)S(1)}, u32[]{:S(2)}, u32[]{:S(2)}) collective-permute-start(bf16[1,128,256]{2,1,0:T(8,128)(2,1)} %bitcast.14), channel_id=1, source_target_pairs={{0,16},{8,24},{16,0},{24,8},{1,17},{9,25},{17,1},{25,9},{2,18},{10... | collective-permute-start | bytes 196616 | tf_op jit(solution)/shard_map/ppermute | solution.py:23
  5.6 0.9 %collective-permute-done.refs_1_ = bf16[1,128,128]{2,1,0:T(8,128)(2,1)S(1)} collective-permute-done((bf16[1,128,128]{2,1,0:T(8,128)(2,1)}, bf16[1,128,128]{2,1,0:T(8,128)(2,1)S(1)}, u32[]{:S(2)}, u32[]{:S(2)}) %collective-permute-start) | collective-permute-done | bytes 32800 | tf_op jit(solution)/shard_map/ppermute | solution.py:23
  6.5 0.8 %pad_maximum_fusion.2 = bf16[2,128,128]{2,1,0:T(8,128)(2,1)S(1)} fusion(bf16[1,128,128]{2,1,0:T(8,128)(2,1)S(1)} %collective-permute-done.refs_1_, bf16[1,128,128]{2,1,0:T(8,128)(2,1)} %bitcast.11), kind=kLoop, calls=%fused_computation.2 | loop fusion | flops 32768 | bytes 131072 | tf_op jit(solution)/shard_map/concatenate | solution.py:29
  7.3 0.0 copy-start
  7.3 0.0 copy-start.6
  7.3 1.6 %collective-permute-start.1 = (bf16[2,128,128]{2,1,0:T(8,128)(2,1)S(1)}, bf16[2,128,128]{2,1,0:T(8,128)(2,1)S(1)}, u32[]{:S(2)}, u32[]{:S(2)}) collective-permute-start(bf16[2,128,128]{2,1,0:T(8,128)(2,1)S(1)} %pad_maximum_fusion.2), channel_id=1, source_target_pairs={{0,2},{1,3},{2,0},{3,1},{4,6},{5,7},{6,4},{7,5},{8,10},{9,11},{10,... | collective-permute-start | bytes 196616 | tf_op jit(solution)/shard_map/ppermute | solution.py:23
  8.9 0.0 collective-permute-done.3.refs_5_
  8.9 0.0 copy-done.1
  8.9 1.6 %collective-permute-start.4 = (bf16[2,128,256]{2,1,0:T(8,128)(2,1)S(1)}, bf16[2,128,256]{2,1,0:T(8,128)(2,1)S(1)}, u32[]{:S(2)}, u32[]{:S(2)}) collective-permute-start(bf16[2,128,256]{2,1,0:T(8,128)(2,1)S(1)} %pad_maximum_fusion.1), channel_id=1, source_target_pairs={{0,8},{8,0},{16,24},{24,16},{1,9},{9,1},{17,25},{25,17},{2,10},{10... | collective-permute-start | bytes 393224 | tf_op jit(solution)/shard_map/ppermute | solution.py:23
  10.5 1.1 %collective-permute-done.1.refs_2_ = bf16[2,128,128]{2,1,0:T(8,128)(2,1)S(1)} collective-permute-done((bf16[2,128,128]{2,1,0:T(8,128)(2,1)S(1)}, bf16[2,128,128]{2,1,0:T(8,128)(2,1)S(1)}, u32[]{:S(2)}, u32[]{:S(2)}) %collective-permute-start.1) | collective-permute-done | bytes 65568 | tf_op jit(solution)/shard_map/ppermute | solution.py:23
  11.6 0.0 copy-done
  11.7 0.1 collective-permute-start.2
  12.4 0.0 copy-done.6
  12.4 0.2 copy.9
  12.6 1.4 %collective-permute-done.4.refs_6_ = bf16[2,128,256]{2,1,0:T(8,128)(2,1)S(1)} collective-permute-done((bf16[2,128,256]{2,1,0:T(8,128)(2,1)S(1)}, bf16[2,128,256]{2,1,0:T(8,128)(2,1)S(1)}, u32[]{:S(2)}, u32[]{:S(2)}) %collective-permute-start.4) | collective-permute-done | bytes 131104 | tf_op jit(solution)/shard_map/ppermute | solution.py:23
  14.0 0.0 collective-permute-done.2.refs_3_
  14.0 0.6 %volume.1 = (bf16[4,4,8,128]{3,2,1,0:T(8,128)(2,1)S(1)}, bf16[3,4,8,128]{3,2,1,0:T(8,128)(2,1)S(1)}, bf16[3,4,8,128]{3,2,1,0:T(8,128)(2,1)S(1)}) custom-call(bf16[1,128,128]{2,1,0:T(8,128)(2,1)S(1)} %bitcast.13, bf16[1,128,128]{2,1,0:T(8,128)(2,1)S(1)} %collective-permute-done.refs_1_, bf16[2,128,128]{2,1,0:T(8,128)(2,1)S(1)} %collective-permute-done.1.refs_2_, ...), custom_call_target="tpu_custom_call" | custom-call | tf_op jit(solution)/shard_map/volume/pallas_call | solution.py:417
  14.6 1.5 %collective-permute-start.5 = (bf16[3,4,8,128]{3,2,1,0:T(8,128)(2,1)S(1)}, bf16[3,4,8,128]{3,2,1,0:T(8,128)(2,1)S(1)}, u32[]{:S(2)}, u32[]{:S(2)}) collective-permute-start(bf16[3,4,8,128]{3,2,1,0:T(8,128)(2,1)S(1)} %get-tuple-element.14), channel_id=1, source_target_pairs={{0,8},{8,16},{16,24},{24,0},{1,9},{9,17},{17,25},{25,1},{2,10},{10... | collective-permute-start | bytes 73736 | tf_op jit(solution)/shard_map/ppermute | solution.py:38
  16.2 1.4 %collective-permute-start.6 = (bf16[3,4,8,128]{3,2,1,0:T(8,128)(2,1)S(1)}, bf16[3,4,8,128]{3,2,1,0:T(8,128)(2,1)S(1)}, u32[]{:S(2)}, u32[]{:S(2)}) collective-permute-start(bf16[3,4,8,128]{3,2,1,0:T(8,128)(2,1)S(1)} %get-tuple-element.15), channel_id=1, source_target_pairs={{8,0},{16,8},{24,16},{0,24},{9,1},{17,9},{25,17},{1,25},{10,2},{18... | collective-permute-start | bytes 73736 | tf_op jit(solution)/shard_map/ppermute | solution.py:38
  17.6 2.4 %collective-permute-done.6.high_a_ref = bf16[3,4,8,128]{3,2,1,0:T(8,128)(2,1)S(1)} collective-permute-done((bf16[3,4,8,128]{3,2,1,0:T(8,128)(2,1)S(1)}, bf16[3,4,8,128]{3,2,1,0:T(8,128)(2,1)S(1)}, u32[]{:S(2)}, u32[]{:S(2)}) %collective-permute-start.6) | collective-permute-done | bytes 24608 | tf_op jit(solution)/shard_map/ppermute | solution.py:38
  20.0 0.0 collective-permute-done.5.low_a_ref
  20.0 0.1 collective-permute-start.7
  20.1 0.0 copy-start.2
  20.1 0.0 copy-start.3
  20.1 3.6 %collective-permute-start.8 = (bf16[10,3,8,128]{3,2,1,0:T(8,128)(2,1)S(1)}, bf16[10,3,8,128]{3,2,1,0:T(8,128)(2,1)S(1)}, u32[]{:S(2)}, u32[]{:S(2)}) collective-permute-start(bf16[10,3,8,128]{3,2,1,0:T(8,128)(2,1)S(1)} %pad_maximum_fusion.4), channel_id=1, source_target_pairs={{1,0},{2,1},{3,2},{4,3},{5,4},{6,5},{7,6},{0,7},{9,8},{10,9},{11,1... | collective-permute-start | bytes 184328 | tf_op jit(solution)/shard_map/ppermute | solution.py:38
  23.7 0.0 copy-start.4
  23.7 0.0 copy-start.5
  23.7 0.0 copy-done.2
  23.7 0.0 copy-done.3
  23.7 0.6 %copy-done.4 = f32[16]{0:T(128)S(1)} copy-done((f32[16]{0:T(128)S(1)}, f32[16]{0:T(128)}, u32[]{:S(2)}) %copy-start.4) | copy-done | bytes 88
  24.4 0.0 copy-done.5
  24.4 1.0 %weights.1 = (f32[3,16,128]{2,1,0:T(8,128)S(1)}, bf16[128,512]{1,0:T(8,128)(2,1)S(1)}, bf16[192,768]{1,0:T(8,128)(2,1)S(1)}, bf16[144,768]{1,0:T(8,128)(2,1)S(1)}) custom-call(f32[16]{0:T(128)S(1)} %copy-done.4, f32[16]{0:T(128)S(1)} %copy-done.5, f32[1]{0:T(128)S(6)} %copy.10.b3_ref, bf16[27,3,16]{2,1,0:T(4,128)(2,1)S(1)} %bitcast.17, ...), custom_call_target="tpu_custom_call" | custom-call | flops 2000000000 | bytes 1000000 | tf_op jit(solution)/shard_map/weights/pallas_call | solution.py:390
  25.3 0.3 collective-permute-done.7.low_b_ref
  25.6 0.0 collective-permute-done.8.high_b_ref
  25.6 6.2 %layers.1 = bf16[4,4,32,32]{3,2,1,0:T(8,128)(2,1)} custom-call(f32[3,16,128]{2,1,0:T(8,128)S(1)} %get-tuple-element.12.bias_ref, bf16[4,4,8,128]{3,2,1,0:T(8,128)(2,1)S(1)} %get-tuple-element.13.own_ref, bf16[3,4,8,128]{3,2,1,0:T(8,128)(2,1)S(1)} %collective-permute-done.5.low_a_ref, bf16[3,4,8,128]{3,2,1,0:T(8,128)(2,1)S(1)} %collective-permute-done.6.high_a_ref, ...), custom_call_target="tpu_custom_call" | custom-call | tf_op jit(solution)/shard_map/layers/pallas_call | solution.py:439
  (7 shorter events, 0.1 us)
Async XLA Ops:
  0.0 6.5 %collective-permute-start = (bf16[1,128,128]{2,1,0:T(8,128)(2,1)}, bf16[1,128,128]{2,1,0:T(8,128)(2,1)S(1)}, u32[]{:S(2)}, u32[]{:S(2)}) collective-permute-start(bf16[1,128,128]{2,1,0:T(8,128)(2,1)} %bitcast.10), channel_id=1, source_target_pairs={{0,4},{1,5},{2,6},{3,7},{4,0},{5,1},{6,2},{7,3},{8,12},{9,13},{10,... | collective-permute-start | bytes 98312 | tf_op jit(solution)/shard_map/ppermute | solution.py:23
  4.1 4.9 %copy-start.1 = (bf16[1,4,32,256]{3,2,1,0:T(8,128)(2,1)S(1)}, bf16[1,4,32,256]{3,2,1,0:T(8,128)(2,1)}, u32[]{:S(2)}) copy-start(bf16[1,4,32,256]{3,2,1,0:T(8,128)(2,1)} %param.9) | copy-start | bytes 196612
  4.1 4.9 %collective-permute-start.3 = (bf16[1,128,256]{2,1,0:T(8,128)(2,1)}, bf16[1,128,256]{2,1,0:T(8,128)(2,1)S(1)}, u32[]{:S(2)}, u32[]{:S(2)}) collective-permute-start(bf16[1,128,256]{2,1,0:T(8,128)(2,1)} %bitcast.14), channel_id=1, source_target_pairs={{0,16},{8,24},{16,0},{24,8},{1,17},{9,25},{17,1},{25,9},{2,18},{10... | collective-permute-start | bytes 196616 | tf_op jit(solution)/shard_map/ppermute | solution.py:23
  7.3 4.4 %copy-start = (bf16[1,4,32,128]{3,2,1,0:T(8,128)(2,1)S(1)}, bf16[1,4,32,128]{3,2,1,0:T(8,128)(2,1)}, u32[]{:S(2)}) copy-start(bf16[1,4,32,128]{3,2,1,0:T(8,128)(2,1)} %param.8) | copy-start | bytes 98308
  7.3 5.1 %copy-start.6 = (bf16[3,3,3,3,16,16]{5,4,3,2,1,0:T(8,128)(2,1)S(1)}, bf16[3,3,3,3,16,16]{5,4,3,2,1,0:T(8,128)(2,1)}, u32[]{:S(2)}) copy-start(bf16[3,3,3,3,16,16]{5,4,3,2,1,0:T(8,128)(2,1)} %param.12) | copy-start | bytes 124420
  7.3 4.3 %collective-permute-start.1 = (bf16[2,128,128]{2,1,0:T(8,128)(2,1)S(1)}, bf16[2,128,128]{2,1,0:T(8,128)(2,1)S(1)}, u32[]{:S(2)}, u32[]{:S(2)}) collective-permute-start(bf16[2,128,128]{2,1,0:T(8,128)(2,1)S(1)} %pad_maximum_fusion.2), channel_id=1, source_target_pairs={{0,2},{1,3},{2,0},{3,1},{4,6},{5,7},{6,4},{7,5},{8,10},{9,11},{10,... | collective-permute-start | bytes 196616 | tf_op jit(solution)/shard_map/ppermute | solution.py:23
  8.9 5.0 %collective-permute-start.4 = (bf16[2,128,256]{2,1,0:T(8,128)(2,1)S(1)}, bf16[2,128,256]{2,1,0:T(8,128)(2,1)S(1)}, u32[]{:S(2)}, u32[]{:S(2)}) collective-permute-start(bf16[2,128,256]{2,1,0:T(8,128)(2,1)S(1)} %pad_maximum_fusion.1), channel_id=1, source_target_pairs={{0,8},{8,0},{16,24},{24,16},{1,9},{9,1},{17,25},{25,17},{2,10},{10... | collective-permute-start | bytes 393224 | tf_op jit(solution)/shard_map/ppermute | solution.py:23
  11.7 2.3 %collective-permute-start.2 = (bf16[4,128,128]{2,1,0:T(8,128)(2,1)S(1)}, bf16[4,128,128]{2,1,0:T(8,128)(2,1)S(1)}, u32[]{:S(2)}, u32[]{:S(2)}) collective-permute-start(bf16[4,128,128]{2,1,0:T(8,128)(2,1)S(1)} %pad_maximum_fusion), channel_id=1, source_target_pairs={{0,1},{1,0},{2,3},{3,2},{4,5},{5,4},{6,7},{7,6},{8,9},{9,8},{10,11... | collective-permute-start | bytes 393224 | tf_op jit(solution)/shard_map/ppermute | solution.py:23
  14.6 5.4 %collective-permute-start.5 = (bf16[3,4,8,128]{3,2,1,0:T(8,128)(2,1)S(1)}, bf16[3,4,8,128]{3,2,1,0:T(8,128)(2,1)S(1)}, u32[]{:S(2)}, u32[]{:S(2)}) collective-permute-start(bf16[3,4,8,128]{3,2,1,0:T(8,128)(2,1)S(1)} %get-tuple-element.14), channel_id=1, source_target_pairs={{0,8},{8,16},{16,24},{24,0},{1,9},{9,17},{17,25},{25,1},{2,10},{10... | collective-permute-start | bytes 73736 | tf_op jit(solution)/shard_map/ppermute | solution.py:38
  16.2 3.8 %collective-permute-start.6 = (bf16[3,4,8,128]{3,2,1,0:T(8,128)(2,1)S(1)}, bf16[3,4,8,128]{3,2,1,0:T(8,128)(2,1)S(1)}, u32[]{:S(2)}, u32[]{:S(2)}) collective-permute-start(bf16[3,4,8,128]{3,2,1,0:T(8,128)(2,1)S(1)} %get-tuple-element.15), channel_id=1, source_target_pairs={{8,0},{16,8},{24,16},{0,24},{9,1},{17,9},{25,17},{1,25},{10,2},{18... | collective-permute-start | bytes 73736 | tf_op jit(solution)/shard_map/ppermute | solution.py:38
  20.0 5.6 %collective-permute-start.7 = (bf16[10,3,8,128]{3,2,1,0:T(8,128)(2,1)S(1)}, bf16[10,3,8,128]{3,2,1,0:T(8,128)(2,1)S(1)}, u32[]{:S(2)}, u32[]{:S(2)}) collective-permute-start(bf16[10,3,8,128]{3,2,1,0:T(8,128)(2,1)S(1)} %pad_maximum_fusion.3), channel_id=1, source_target_pairs={{0,1},{1,2},{2,3},{3,4},{4,5},{5,6},{6,7},{7,0},{8,9},{9,10},{10,1... | collective-permute-start | bytes 184328 | tf_op jit(solution)/shard_map/ppermute | solution.py:38
  20.1 3.6 %copy-start.2 = (bf16[3,3,3,3,1,16]{5,3,4,2,1,0:T(4,128)(2,1)S(1)}, bf16[3,3,3,3,1,16]{5,3,4,2,1,0:T(4,128)(2,1)}, u32[]{:S(2)}) copy-start(bf16[3,3,3,3,1,16]{5,3,4,2,1,0:T(4,128)(2,1)} %param.10) | copy-start | bytes 7780
  20.1 3.6 %copy-start.3 = (bf16[3,3,3,3,16,1]{4,3,5,2,1,0:T(4,128)(2,1)S(1)}, bf16[3,3,3,3,16,1]{4,3,5,2,1,0:T(4,128)(2,1)}, u32[]{:S(2)}) copy-start(bf16[3,3,3,3,16,1]{4,3,5,2,1,0:T(4,128)(2,1)} %param.14) | copy-start | bytes 7780
  20.1 5.5 %collective-permute-start.8 = (bf16[10,3,8,128]{3,2,1,0:T(8,128)(2,1)S(1)}, bf16[10,3,8,128]{3,2,1,0:T(8,128)(2,1)S(1)}, u32[]{:S(2)}, u32[]{:S(2)}) collective-permute-start(bf16[10,3,8,128]{3,2,1,0:T(8,128)(2,1)S(1)} %pad_maximum_fusion.4), channel_id=1, source_target_pairs={{1,0},{2,1},{3,2},{4,3},{5,4},{6,5},{7,6},{0,7},{9,8},{10,9},{11,1... | collective-permute-start | bytes 184328 | tf_op jit(solution)/shard_map/ppermute | solution.py:38
  23.7 0.7 %copy-start.4 = (f32[16]{0:T(128)S(1)}, f32[16]{0:T(128)}, u32[]{:S(2)}) copy-start(f32[16]{0:T(128)} %b1_ref.1) | copy-start | bytes 196
  23.7 0.7 %copy-start.5 = (f32[16]{0:T(128)S(1)}, f32[16]{0:T(128)}, u32[]{:S(2)}) copy-start(f32[16]{0:T(128)} %b2_ref.1) | copy-start | bytes 196

commit v3 on v2

--- a/solution.py
+++ b/solution.py
@@ -11,6 +11,22 @@
 TAPS = 3
 HALO = 3
 epsilon = 1e-06
+
+
+def copy_kernel(in_ref, out_ref):
+    out_ref[...] = in_ref[...]
+
+
+def on_chip(block):
+    return pl.pallas_call(
+        copy_kernel,
+        out_shape=jax.ShapeDtypeStruct(block.shape, block.dtype),
+        in_specs=[pl.BlockSpec(memory_space=pltpu.VMEM)],
+        out_specs=pl.BlockSpec(memory_space=pltpu.VMEM),
+        cost_estimate=pl.CostEstimate(flops=1_000_000_000, bytes_accessed=0, transcendentals=0),
+        compiler_params=pltpu.CompilerParams(vmem_limit_bytes=4 << 20),
+        name="own",
+    )(block)
 
 
 def xor_blocks(block, axis):
@@ -21,6 +37,8 @@
     while step:
         swap = [(i, i ^ step) for i in range(count)]
         got = lax.ppermute(held, axis, swap)
+        if len(masks) == 1:
+            held = on_chip(held)
         got_masks = [m ^ step for m in masks]
         pieces.append(got)
         piece_masks.append(got_masks)
@@ -93,6 +111,13 @@
                 high_ref[i - rows_a + HALO, k] = plane
 
 
+def first_tiles():
+    tiles = [(0, ((a, e, 0), (a, e, 1))) for a in range(TAPS) for e in range(TAPS)]
+    tiles += [(1, ((a, 0, 2), (a, 1, 2))) for a in range(TAPS)]
+    tiles += [(2, ((0, 2, 2), (1, 2, 2))), (1, ((2, 2, 2), None))]
+    return tiles
+
+
 def weights_kernel(
     b1_ref, b2_ref, b3_ref, one_ref, two_ref, three_ref, bias_ref, w1_ref, w2_ref, w3_ref, w3_s,
     *, inner, rows_a, rows_b,
@@ -117,20 +142,27 @@
         return ((a * TAPS + b) * TAPS + e) * TAPS + g
 
     one = [tiled(one_ref[:, g, :]) for g in range(TAPS)]
-    column = jnp.where(row < inner, row, jnp.where(row == inner, inner, -2))
-    column = jnp.where(row == 2 * inner - 1, -1, column)
-    slabs = []
-    for a in range(TAPS):
-        for e in range(TAPS):
-            for g in range(TAPS):
-                slab = jnp.zeros((channels, LANES), jnp.float32)
-                for b in range(TAPS):
-                    n = tap(a, b, e, 0) // TAPS
-                    hit = (column - lane_block == b - 1) & (column >= -1)
-                    slab = jnp.where(hit, one[g][n : n + 1], slab)
-                slabs.append(slab)
-    while (len(slabs) * channels) % LANES:
-        slabs.append(jnp.zeros((channels, LANES), jnp.float32))
+    column = lax.broadcasted_iota(jnp.int32, (inner, LANES), 0)
+    half_block = lax.broadcasted_iota(jnp.int32, (inner, LANES), 1) // channels
+
+    def half_slab(part):
+        main = jnp.zeros((inner, LANES), jnp.float32)
+        side = jnp.zeros((inner, LANES), jnp.float32)
+        if part is not None:
+            a, e, g = part
+            for b in range(TAPS):
+                n = tap(a, b, e, 0) // TAPS
+                value = one[g][n : n + 1]
+                main = jnp.where(column - half_block == b - 1, value, main)
+                if b == 0:
+                    side = jnp.where((column == inner - 1) & (half_block == 0), value, side)
+                if b == TAPS - 1:
+                    side = jnp.where((column == 0) & (half_block == 1), value, side)
+        return jnp.concatenate([main, side], axis=1)
+
+    slabs = [half_slab(part) for _, parts in first_tiles() for part in parts]
+    while (len(slabs) * inner) % LANES:
+        slabs.append(jnp.zeros((inner, 2 * LANES), jnp.float32))
     w1_ref[...] = jnp.concatenate(slabs, axis=0).T.astype(jnp.bfloat16)
 
     two = tiled(two_ref[...])
@@ -207,23 +239,19 @@
         pos = lanes(x.shape[0]) % size
         return jnp.where(pos < size - step, pltpu.roll(x, LANES - step, 1), 0.0)
 
-    plane_row = lax.broadcasted_iota(jnp.int32, (inner, LANES), 0)
-
-    def spread_row(a):
+    above = None
+    for a in range(ext_a):
+        shifted = []
         for b in range(ext_b):
-            x = plane(a, b).astype(jnp.float32)
-            x = jnp.where(inside(a, b, HALO), x, 0.0)
-            before = up(x, tgt_cols, LANES)
-            after = down(x, tgt_cols, LANES)
-            edge = jnp.where(plane_row == inner - 1, before, jnp.where(plane_row == 0, after, 0.0))
-            both = jnp.concatenate([x, edge], axis=0)
-            rows = 2 * inner
-            vj[a, b, 0:rows] = up(both, 1, tgt_cols).astype(jnp.bfloat16)
-            vj[a, b, rows : 2 * rows] = both.astype(jnp.bfloat16)
-            vj[a, b, 2 * rows : 3 * rows] = down(both, 1, tgt_cols).astype(jnp.bfloat16)
-
-    for a in range(ext_a):
-        spread_row(a)
+            x = jnp.where(inside(a, b, HALO), plane(a, b).astype(jnp.float32), 0.0)
+            vj[0, a, b] = jnp.concatenate([up(x, 1, tgt_cols), x], axis=0).astype(jnp.bfloat16)
+            shifted.append(down(x, 1, tgt_cols))
+        for b in range(ext_b):
+            beside = shifted[b + 1] if b + 1 < ext_b else jnp.zeros_like(shifted[b])
+            vj[1, a, b] = jnp.concatenate([shifted[b], beside], axis=0).astype(jnp.bfloat16)
+            if above is not None:
+                vj[2, a - 1, b] = jnp.concatenate([above[b], shifted[b]], axis=0).astype(jnp.bfloat16)
+        above = shifted
 
     def put(dst, a, b, blocks):
         dst[a, b, 0:channels] = up(blocks[-1], tgt_cols, LANES).astype(jnp.bfloat16)
@@ -233,7 +261,8 @@
 
     l1_a, l1_b = ext_a - 2, ext_b - 2
     bias1 = bias_ref[0]
-    depth1 = TAPS * TAPS * TAPS * 2 * inner
+    depth1 = len(first_tiles()) * 2 * inner
+    rows1 = (inner + 2) * channels
     group = 4 if l1_b % 4 == 0 else 2
 
     def first_row(a):
@@ -241,27 +270,24 @@
             x = jnp.concatenate(
                 [
                     jnp.concatenate(
-                        [vj[a + da, b0 + n + db] for da in range(TAPS) for db in range(TAPS)], axis=0
+                        [
+                            vj[kind, a + parts[0][0], b0 + n + parts[0][1]]
+                            for kind, parts in first_tiles()
+                        ],
+                        axis=0,
                     )
                     for n in range(group)
                 ],
                 axis=1,
             )
-            got = jnp.dot(w1_ref[:, :depth1], x, preferred_element_type=jnp.float32)
+            got = jnp.dot(w1_ref[:rows1, :depth1], x, preferred_element_type=jnp.float32)
             for n in range(group):
                 ok = inside(a, b0 + n, HALO - 1)
-                blocks = [
-                    jnp.where(
-                        ok,
-                        jnp.maximum(
-                            got[c * channels : (c + 1) * channels, n * LANES : (n + 1) * LANES]
-                            + bias1,
-                            0.0,
-                        ),
-                        0.0,
-                    )
-                    for c in range(inner)
-                ]
+                part = got[:, n * LANES : (n + 1) * LANES]
+                sums = [part[c * channels : (c + 1) * channels] for c in range(inner + 2)]
+                sums[0] = sums[0] + up(sums[inner], tgt_cols, LANES)
+                sums[inner - 1] = sums[inner - 1] + down(sums[inner + 1], tgt_cols, LANES)
+                blocks = [jnp.where(ok, jnp.maximum(x + bias1, 0.0), 0.0) for x in sums[:inner]]
                 put(a1, a, b0 + n, blocks)
 
     for a in range(l1_a):
@@ -386,12 +412,12 @@
     taps = TAPS**4
     w3_cols = (rows_a + 2) * LANES
     w3_rows = TAPS * TAPS * rows_a * rows_b
-    w1_cols = -(-(TAPS**3 * channels) // LANES) * LANES
+    w1_cols = -(-(len(first_tiles()) * 2 * inner) // LANES) * LANES
     biases, w1, w2, w3 = pl.pallas_call(
         partial(weights_kernel, inner=inner, rows_a=rows_a, rows_b=rows_b),
         out_shape=(
             jax.ShapeDtypeStruct((TAPS, channels, LANES), jnp.float32),
-            jax.ShapeDtypeStruct((LANES, w1_cols), jnp.bfloat16),
+            jax.ShapeDtypeStruct((2 * LANES, w1_cols), jnp.bfloat16),
             jax.ShapeDtypeStruct((TAPS * 4 * channels, TAPS * 2 * LANES), jnp.bfloat16),
             jax.ShapeDtypeStruct((w3_rows, w3_cols), jnp.bfloat16),
         ),
@@ -448,7 +474,7 @@
         in_specs=[VMEM] * 9,
         out_specs=VMEM,
         scratch_shapes=[
-            pltpu.VMEM((ext_a, ext_b, TAPS * 2 * inner, LANES), jnp.bfloat16),
+            pltpu.VMEM((TAPS, ext_a, ext_b, 2 * inner, LANES), jnp.bfloat16),
             pltpu.VMEM((ext_a - 2, ext_b - 2, (inner + 2) * channels, LANES), jnp.bfloat16),
             pltpu.VMEM((ext_a - 4, ext_b - 4, inner * channels, LANES), jnp.bfloat16),
         ],

time: 32 us -> 30.7 us (0.959)
  Pallas kernels: 7.76 us -> 6.78 us
  other arithmetic: 0.82 us -> 0.06 us
  local copies, waits for them, and re-layouts: 0.91 us -> 1.67 us
  waiting for transfers between devices: 6.13 us -> 5.67 us
    pallas_call x1, Pallas kernels: 6.18 us -> 5.19 us  [one_pair(): pl.pallas_call(partial(layers_kernel, sizes=(lax.axis_size('src'), lax.ax...]
    unnamed x14 -> x16, local copies, waits for them, and re-layouts: 0.69 us -> 1.45 us
    concatenate x3, other arithmetic: 0.79 us -> 0.04 us  [xor_blocks(): held = jnp.concatenate([held, got], axis=0)]
    ppermute x5, waiting for transfers between devices: 3.45 us -> 3.05 us  [xor_blocks(): got = lax.ppermute(held, axis, swap)]
  transfers between devices with their start and end apart: 9 -> 9, of which waited for: 5 -> 6; matrix products, arithmetic and copies ran while one was open for 3% -> 1% of each run, Pallas kernels for 3% -> 3%
where the time goes in v3:
time: 30.7 us; the launch traced here: 30.4 us
  starting transfers between devices  15.4 us (50%)
  Pallas kernels  6.78 us (22%)
  waiting for transfers between devices  5.67 us (18%)
  local copies, waits for them, and re-layouts  1.67 us (5%)
  between operations  0.78 us (3%)
    ppermute x5, starting transfers between devices, xor_blocks(): got = lax.ppermute(held, axis, swap)  8.84 us
    pallas_call x1, Pallas kernels, one_pair(): pl.pallas_call(partial(layers_kernel, sizes=(lax.axis_size('src'), lax.ax...  5.19 us
    ppermute x2, starting transfers between devices, swap_edges(): lax.ppermute(low_edge, axis, backward)  4.99 us
    ppermute x5, waiting for transfers between devices, xor_blocks(): got = lax.ppermute(held, axis, swap)  3.05 us
    ppermute x2, waiting for transfers between devices, swap_edges(): lax.ppermute(low_edge, axis, backward)  2.38 us
    ppermute x2, starting transfers between devices, swap_edges(): lax.ppermute(high_edge, axis, forward)  1.6 us
    unnamed x16, local copies, waits for them, and re-layouts  1.45 us
    pallas_call x1, Pallas kernels, one_pair(): pl.pallas_call(partial(weights_kernel, inner=inner, rows_a=rows_a, rows_b...  0.96 us
  transfers between devices with their start and end apart: 9, of which 6 were waited for; matrix products, arithmetic and copies ran while one was open for 1% of the time, Pallas kernels for 3%

profile of v3, /device:TPU:0, one launch (start us, length us, event | category | flops | bytes accessed | tf_op | source)
XLA Modules:
  0.0 30.4 jit_solution(2987435107175214038)
XLA Ops:
  0.0 4.1 %collective-permute-start = (bf16[1,128,128]{2,1,0:T(8,128)(2,1)}, bf16[1,128,128]{2,1,0:T(8,128)(2,1)S(1)}, u32[]{:S(2)}, u32[]{:S(2)}) collective-permute-start(bf16[1,128,128]{2,1,0:T(8,128)(2,1)} %bitcast.13), channel_id=1, source_target_pairs={{0,4},{1,5},{2,6},{3,7},{4,0},{5,1},{6,2},{7,3},{8,12},{9,13},{10,... | collective-permute-start | bytes 98312 | tf_op jit(solution)/shard_map/ppermute | solution.py:39
  4.1 0.0 copy-start
  4.1 1.5 %collective-permute-start.3 = (bf16[1,128,256]{2,1,0:T(8,128)(2,1)}, bf16[1,128,256]{2,1,0:T(8,128)(2,1)S(1)}, u32[]{:S(2)}, u32[]{:S(2)}) collective-permute-start(bf16[1,128,256]{2,1,0:T(8,128)(2,1)} %bitcast.10), channel_id=1, source_target_pairs={{0,16},{8,24},{16,0},{24,8},{1,17},{9,25},{17,1},{25,9},{2,18},{10... | collective-permute-start | bytes 196616 | tf_op jit(solution)/shard_map/ppermute | solution.py:39
  5.6 0.0 copy-start.1
  5.6 0.8 %copy-done.1 = bf16[1,4,32,128]{3,2,1,0:T(8,128)(2,1)S(1)} copy-done((bf16[1,4,32,128]{3,2,1,0:T(8,128)(2,1)S(1)}, bf16[1,4,32,128]{3,2,1,0:T(8,128)(2,1)}, u32[]{:S(2)}) %copy-start.1) | copy-done | bytes 32792
  6.3 0.0 copy-done
  6.4 0.0 copy-start.7
  6.4 0.1 collective-permute-done.refs_1_
  6.5 1.6 %collective-permute-start.1 = (bf16[2,128,128]{2,1,0:T(8,128)(2,1)S(1)}, bf16[2,128,128]{2,1,0:T(8,128)(2,1)S(1)}, u32[]{:S(2)}, u32[]{:S(2)}) collective-permute-start(bf16[2,128,128]{2,1,0:T(8,128)(2,1)S(1)} %pad_maximum_fusion.2), channel_id=1, source_target_pairs={{0,2},{1,3},{2,0},{3,1},{4,6},{5,7},{6,4},{7,5},{8,10},{9,11},{10,... | collective-permute-start | bytes 196616 | tf_op jit(solution)/shard_map/ppermute | solution.py:39
  8.2 0.4 %collective-permute-done.3.refs_5_ = bf16[1,128,256]{2,1,0:T(8,128)(2,1)S(1)} collective-permute-done((bf16[1,128,256]{2,1,0:T(8,128)(2,1)}, bf16[1,128,256]{2,1,0:T(8,128)(2,1)S(1)}, u32[]{:S(2)}, u32[]{:S(2)}) %collective-permute-start.3) | collective-permute-done | bytes 65568 | tf_op jit(solution)/shard_map/ppermute | solution.py:39
  8.6 1.6 %collective-permute-start.4 = (bf16[2,128,256]{2,1,0:T(8,128)(2,1)S(1)}, bf16[2,128,256]{2,1,0:T(8,128)(2,1)S(1)}, u32[]{:S(2)}, u32[]{:S(2)}) collective-permute-start(bf16[2,128,256]{2,1,0:T(8,128)(2,1)S(1)} %pad_maximum_fusion.1), channel_id=1, source_target_pairs={{0,8},{8,0},{16,24},{24,16},{1,9},{9,1},{17,25},{25,17},{2,10},{10... | collective-permute-start | bytes 393224 | tf_op jit(solution)/shard_map/ppermute | solution.py:39
  10.1 0.7 %collective-permute-done.1.refs_2_ = bf16[2,128,128]{2,1,0:T(8,128)(2,1)S(1)} collective-permute-done((bf16[2,128,128]{2,1,0:T(8,128)(2,1)S(1)}, bf16[2,128,128]{2,1,0:T(8,128)(2,1)S(1)}, u32[]{:S(2)}, u32[]{:S(2)}) %collective-permute-start.1) | collective-permute-done | bytes 65568 | tf_op jit(solution)/shard_map/ppermute | solution.py:39
  10.9 0.1 collective-permute-start.2
  11.6 0.0 copy-done.7
  11.6 0.0 copy-start.2
  11.6 0.2 copy.9
  11.8 1.8 %collective-permute-done.4.refs_6_ = bf16[2,128,256]{2,1,0:T(8,128)(2,1)S(1)} collective-permute-done((bf16[2,128,256]{2,1,0:T(8,128)(2,1)S(1)}, bf16[2,128,256]{2,1,0:T(8,128)(2,1)S(1)}, u32[]{:S(2)}, u32[]{:S(2)}) %collective-permute-start.4) | collective-permute-done | bytes 131104 | tf_op jit(solution)/shard_map/ppermute | solution.py:39
  13.6 0.0 collective-permute-done.2.refs_3_
  13.6 0.0 copy-done.2
  13.6 0.6 %volume.1 = (bf16[4,4,8,128]{3,2,1,0:T(8,128)(2,1)S(1)}, bf16[3,4,8,128]{3,2,1,0:T(8,128)(2,1)S(1)}, bf16[3,4,8,128]{3,2,1,0:T(8,128)(2,1)S(1)}) custom-call(bf16[1,128,128]{2,1,0:T(8,128)(2,1)S(1)} %bitcast.15, bf16[1,128,128]{2,1,0:T(8,128)(2,1)S(1)} %collective-permute-done.refs_1_, bf16[2,128,128]{2,1,0:T(8,128)(2,1)S(1)} %collective-permute-done.1.refs_2_, ...), custom_call_target="tpu_custom_call" | custom-call | tf_op jit(solution)/shard_map/volume/pallas_call | solution.py:443
  14.2 1.5 %collective-permute-start.5 = (bf16[3,4,8,128]{3,2,1,0:T(8,128)(2,1)S(1)}, bf16[3,4,8,128]{3,2,1,0:T(8,128)(2,1)S(1)}, u32[]{:S(2)}, u32[]{:S(2)}) collective-permute-start(bf16[3,4,8,128]{3,2,1,0:T(8,128)(2,1)S(1)} %get-tuple-element.14), channel_id=1, source_target_pairs={{0,8},{8,16},{16,24},{24,0},{1,9},{9,17},{17,25},{25,1},{2,10},{10... | collective-permute-start | bytes 73736 | tf_op jit(solution)/shard_map/ppermute | solution.py:56
  15.8 1.4 %collective-permute-start.6 = (bf16[3,4,8,128]{3,2,1,0:T(8,128)(2,1)S(1)}, bf16[3,4,8,128]{3,2,1,0:T(8,128)(2,1)S(1)}, u32[]{:S(2)}, u32[]{:S(2)}) collective-permute-start(bf16[3,4,8,128]{3,2,1,0:T(8,128)(2,1)S(1)} %get-tuple-element.15), channel_id=1, source_target_pairs={{8,0},{16,8},{24,16},{0,24},{9,1},{17,9},{25,17},{1,25},{10,2},{18... | collective-permute-start | bytes 73736 | tf_op jit(solution)/shard_map/ppermute | solution.py:56
  17.2 2.4 %collective-permute-done.6.high_a_ref = bf16[3,4,8,128]{3,2,1,0:T(8,128)(2,1)S(1)} collective-permute-done((bf16[3,4,8,128]{3,2,1,0:T(8,128)(2,1)S(1)}, bf16[3,4,8,128]{3,2,1,0:T(8,128)(2,1)S(1)}, u32[]{:S(2)}, u32[]{:S(2)}) %collective-permute-start.6) | collective-permute-done | bytes 24608 | tf_op jit(solution)/shard_map/ppermute | solution.py:56
  19.6 0.0 collective-permute-done.5.low_a_ref
  19.6 0.1 collective-permute-start.7
  19.7 0.0 copy-start.3
  19.7 0.0 copy-start.4
  19.8 3.6 %collective-permute-start.8 = (bf16[10,3,8,128]{3,2,1,0:T(8,128)(2,1)S(1)}, bf16[10,3,8,128]{3,2,1,0:T(8,128)(2,1)S(1)}, u32[]{:S(2)}, u32[]{:S(2)}) collective-permute-start(bf16[10,3,8,128]{3,2,1,0:T(8,128)(2,1)S(1)} %pad_maximum_fusion.4), channel_id=1, source_target_pairs={{1,0},{2,1},{3,2},{4,3},{5,4},{6,5},{7,6},{0,7},{9,8},{10,9},{11,1... | collective-permute-start | bytes 184328 | tf_op jit(solution)/shard_map/ppermute | solution.py:56
  23.3 0.0 copy-start.5
  23.3 0.0 copy-start.6
  23.3 0.0 copy-done.3
  23.3 0.0 copy-done.4
  23.3 0.6 %copy-done.5 = f32[16]{0:T(128)S(1)} copy-done((f32[16]{0:T(128)S(1)}, f32[16]{0:T(128)}, u32[]{:S(2)}) %copy-start.5) | copy-done | bytes 88
  24.0 0.0 copy-done.6
  24.0 1.0 %weights.1 = (f32[3,16,128]{2,1,0:T(8,128)S(1)}, bf16[256,256]{1,0:T(8,128)(2,1)S(1)}, bf16[192,768]{1,0:T(8,128)(2,1)S(1)}, bf16[144,768]{1,0:T(8,128)(2,1)S(1)}) custom-call(f32[16]{0:T(128)S(1)} %copy-done.5, f32[16]{0:T(128)S(1)} %copy-done.6, f32[1]{0:T(128)S(6)} %copy.10.b3_ref, bf16[27,3,16]{2,1,0:T(4,128)(2,1)S(1)} %bitcast.16, ...), custom_call_target="tpu_custom_call" | custom-call | flops 2000000000 | bytes 1000000 | tf_op jit(solution)/shard_map/weights/pallas_call | solution.py:416
  25.0 0.2 collective-permute-done.7.low_b_ref
  25.2 0.0 collective-permute-done.8.high_b_ref
  25.2 5.2 %layers.1 = bf16[4,4,32,32]{3,2,1,0:T(8,128)(2,1)} custom-call(f32[3,16,128]{2,1,0:T(8,128)S(1)} %get-tuple-element.12.bias_ref, bf16[4,4,8,128]{3,2,1,0:T(8,128)(2,1)S(1)} %get-tuple-element.13.own_ref, bf16[3,4,8,128]{3,2,1,0:T(8,128)(2,1)S(1)} %collective-permute-done.5.low_a_ref, bf16[3,4,8,128]{3,2,1,0:T(8,128)(2,1)S(1)} %collective-permute-done.6.high_a_ref, ...), custom_call_target="tpu_custom_call" | custom-call | tf_op jit(solution)/shard_map/layers/pallas_call | solution.py:465
  (10 shorter events, 0.1 us)
Async XLA Ops:
  0.0 6.5 %collective-permute-start = (bf16[1,128,128]{2,1,0:T(8,128)(2,1)}, bf16[1,128,128]{2,1,0:T(8,128)(2,1)S(1)}, u32[]{:S(2)}, u32[]{:S(2)}) collective-permute-start(bf16[1,128,128]{2,1,0:T(8,128)(2,1)} %bitcast.13), channel_id=1, source_target_pairs={{0,4},{1,5},{2,6},{3,7},{4,0},{5,1},{6,2},{7,3},{8,12},{9,13},{10,... | collective-permute-start | bytes 98312 | tf_op jit(solution)/shard_map/ppermute | solution.py:39
  4.1 2.3 %copy-start = (bf16[1,4,32,256]{3,2,1,0:T(8,128)(2,1)S(1)}, bf16[1,4,32,256]{3,2,1,0:T(8,128)(2,1)}, u32[]{:S(2)}) copy-start(bf16[1,4,32,256]{3,2,1,0:T(8,128)(2,1)} %param.9) | copy-start | bytes 196612
  4.1 4.5 %collective-permute-start.3 = (bf16[1,128,256]{2,1,0:T(8,128)(2,1)}, bf16[1,128,256]{2,1,0:T(8,128)(2,1)S(1)}, u32[]{:S(2)}, u32[]{:S(2)}) collective-permute-start(bf16[1,128,256]{2,1,0:T(8,128)(2,1)} %bitcast.10), channel_id=1, source_target_pairs={{0,16},{8,24},{16,0},{24,8},{1,17},{9,25},{17,1},{25,9},{2,18},{10... | collective-permute-start | bytes 196616 | tf_op jit(solution)/shard_map/ppermute | solution.py:39
  5.6 0.8 %copy-start.1 = (bf16[1,4,32,128]{3,2,1,0:T(8,128)(2,1)S(1)}, bf16[1,4,32,128]{3,2,1,0:T(8,128)(2,1)}, u32[]{:S(2)}) copy-start(bf16[1,4,32,128]{3,2,1,0:T(8,128)(2,1)} %param.8) | copy-start | bytes 98308
  6.4 5.2 %copy-start.7 = (bf16[3,3,3,3,16,16]{5,4,3,2,1,0:T(8,128)(2,1)S(1)}, bf16[3,3,3,3,16,16]{5,4,3,2,1,0:T(8,128)(2,1)}, u32[]{:S(2)}) copy-start(bf16[3,3,3,3,16,16]{5,4,3,2,1,0:T(8,128)(2,1)} %param.12) | copy-start | bytes 124420
  6.5 4.3 %collective-permute-start.1 = (bf16[2,128,128]{2,1,0:T(8,128)(2,1)S(1)}, bf16[2,128,128]{2,1,0:T(8,128)(2,1)S(1)}, u32[]{:S(2)}, u32[]{:S(2)}) collective-permute-start(bf16[2,128,128]{2,1,0:T(8,128)(2,1)S(1)} %pad_maximum_fusion.2), channel_id=1, source_target_pairs={{0,2},{1,3},{2,0},{3,1},{4,6},{5,7},{6,4},{7,5},{8,10},{9,11},{10,... | collective-permute-start | bytes 196616 | tf_op jit(solution)/shard_map/ppermute | solution.py:39
  8.6 5.0 %collective-permute-start.4 = (bf16[2,128,256]{2,1,0:T(8,128)(2,1)S(1)}, bf16[2,128,256]{2,1,0:T(8,128)(2,1)S(1)}, u32[]{:S(2)}, u32[]{:S(2)}) collective-permute-start(bf16[2,128,256]{2,1,0:T(8,128)(2,1)S(1)} %pad_maximum_fusion.1), channel_id=1, source_target_pairs={{0,8},{8,0},{16,24},{24,16},{1,9},{9,1},{17,25},{25,17},{2,10},{10... | collective-permute-start | bytes 393224 | tf_op jit(solution)/shard_map/ppermute | solution.py:39
  10.9 2.7 %collective-permute-start.2 = (bf16[4,128,128]{2,1,0:T(8,128)(2,1)S(1)}, bf16[4,128,128]{2,1,0:T(8,128)(2,1)S(1)}, u32[]{:S(2)}, u32[]{:S(2)}) collective-permute-start(bf16[4,128,128]{2,1,0:T(8,128)(2,1)S(1)} %pad_maximum_fusion), channel_id=1, source_target_pairs={{0,1},{1,0},{2,3},{3,2},{4,5},{5,4},{6,7},{7,6},{8,9},{9,8},{10,11... | collective-permute-start | bytes 393224 | tf_op jit(solution)/shard_map/ppermute | solution.py:39
  11.6 2.0 %copy-start.2 = (bf16[1,4,32,128]{3,2,1,0:T(8,128)(2,1)S(1)}, bf16[1,4,32,128]{3,2,1,0:T(8,128)(2,1)}, u32[]{:S(2)}) copy-start(bf16[1,4,32,128]{3,2,1,0:T(8,128)(2,1)} %param.8) | copy-start | bytes 98308
  14.2 5.4 %collective-permute-start.5 = (bf16[3,4,8,128]{3,2,1,0:T(8,128)(2,1)S(1)}, bf16[3,4,8,128]{3,2,1,0:T(8,128)(2,1)S(1)}, u32[]{:S(2)}, u32[]{:S(2)}) collective-permute-start(bf16[3,4,8,128]{3,2,1,0:T(8,128)(2,1)S(1)} %get-tuple-element.14), channel_id=1, source_target_pairs={{0,8},{8,16},{16,24},{24,0},{1,9},{9,17},{17,25},{25,1},{2,10},{10... | collective-permute-start | bytes 73736 | tf_op jit(solution)/shard_map/ppermute | solution.py:56
  15.8 3.8 %collective-permute-start.6 = (bf16[3,4,8,128]{3,2,1,0:T(8,128)(2,1)S(1)}, bf16[3,4,8,128]{3,2,1,0:T(8,128)(2,1)S(1)}, u32[]{:S(2)}, u32[]{:S(2)}) collective-permute-start(bf16[3,4,8,128]{3,2,1,0:T(8,128)(2,1)S(1)} %get-tuple-element.15), channel_id=1, source_target_pairs={{8,0},{16,8},{24,16},{0,24},{9,1},{17,9},{25,17},{1,25},{10,2},{18... | collective-permute-start | bytes 73736 | tf_op jit(solution)/shard_map/ppermute | solution.py:56
  19.6 5.6 %collective-permute-start.7 = (bf16[10,3,8,128]{3,2,1,0:T(8,128)(2,1)S(1)}, bf16[10,3,8,128]{3,2,1,0:T(8,128)(2,1)S(1)}, u32[]{:S(2)}, u32[]{:S(2)}) collective-permute-start(bf16[10,3,8,128]{3,2,1,0:T(8,128)(2,1)S(1)} %pad_maximum_fusion.3), channel_id=1, source_target_pairs={{0,1},{1,2},{2,3},{3,4},{4,5},{5,6},{6,7},{7,0},{8,9},{9,10},{10,1... | collective-permute-start | bytes 184328 | tf_op jit(solution)/shard_map/ppermute | solution.py:56
  19.7 3.6 %copy-start.3 = (bf16[3,3,3,3,1,16]{5,3,4,2,1,0:T(4,128)(2,1)S(1)}, bf16[3,3,3,3,1,16]{5,3,4,2,1,0:T(4,128)(2,1)}, u32[]{:S(2)}) copy-start(bf16[3,3,3,3,1,16]{5,3,4,2,1,0:T(4,128)(2,1)} %param.10) | copy-start | bytes 7780
  19.7 3.6 %copy-start.4 = (bf16[3,3,3,3,16,1]{4,3,5,2,1,0:T(4,128)(2,1)S(1)}, bf16[3,3,3,3,16,1]{4,3,5,2,1,0:T(4,128)(2,1)}, u32[]{:S(2)}) copy-start(bf16[3,3,3,3,16,1]{4,3,5,2,1,0:T(4,128)(2,1)} %param.14) | copy-start | bytes 7780
  19.8 5.4 %collective-permute-start.8 = (bf16[10,3,8,128]{3,2,1,0:T(8,128)(2,1)S(1)}, bf16[10,3,8,128]{3,2,1,0:T(8,128)(2,1)S(1)}, u32[]{:S(2)}, u32[]{:S(2)}) collective-permute-start(bf16[10,3,8,128]{3,2,1,0:T(8,128)(2,1)S(1)} %pad_maximum_fusion.4), channel_id=1, source_target_pairs={{1,0},{2,1},{3,2},{4,3},{5,4},{6,5},{7,6},{0,7},{9,8},{10,9},{11,1... | collective-permute-start | bytes 184328 | tf_op jit(solution)/shard_map/ppermute | solution.py:56
  23.3 0.7 %copy-start.5 = (f32[16]{0:T(128)S(1)}, f32[16]{0:T(128)}, u32[]{:S(2)}) copy-start(f32[16]{0:T(128)} %b1_ref.1) | copy-start | bytes 196
  23.3 0.7 %copy-start.6 = (f32[16]{0:T(128)S(1)}, f32[16]{0:T(128)}, u32[]{:S(2)}) copy-start(f32[16]{0:T(128)} %b2_ref.1) | copy-start | bytes 196

commit v4 on v3

--- a/solution.py
+++ b/solution.py
@@ -39,6 +39,7 @@
         got = lax.ppermute(held, axis, swap)
         if len(masks) == 1:
             held = on_chip(held)
+            pieces[0] = held
         got_masks = [m ^ step for m in masks]
         pieces.append(got)
         piece_masks.append(got_masks)

time: 30.7 us -> 30.6 us (level)
    unnamed x16 -> x14, local copies, waits for them, and re-layouts: 1.45 us -> 1.44 us
where the time goes in v4:
time: 30.6 us; the launch traced here: 30.4 us
  starting transfers between devices  15.4 us (50%)
  Pallas kernels  6.78 us (22%)
  waiting for transfers between devices  5.69 us (19%)
  local copies, waits for them, and re-layouts  1.66 us (5%)
  between operations  0.78 us (3%)
    ppermute x5, starting transfers between devices, xor_blocks(): got = lax.ppermute(held, axis, swap)  8.84 us
    pallas_call x1, Pallas kernels, one_pair(): pl.pallas_call(partial(layers_kernel, sizes=(lax.axis_size('src'), lax.ax...  5.19 us
    ppermute x2, starting transfers between devices, swap_edges(): lax.ppermute(low_edge, axis, backward)  4.98 us
    ppermute x5, waiting for transfers between devices, xor_blocks(): got = lax.ppermute(held, axis, swap)  3.06 us
    ppermute x2, waiting for transfers between devices, swap_edges(): lax.ppermute(low_edge, axis, backward)  2.39 us
    ppermute x2, starting transfers between devices, swap_edges(): lax.ppermute(high_edge, axis, forward)  1.61 us
    unnamed x14, local copies, waits for them, and re-layouts  1.44 us
    pallas_call x1, Pallas kernels, one_pair(): pl.pallas_call(partial(weights_kernel, inner=inner, rows_a=rows_a, rows_b...  0.96 us
  transfers between devices with their start and end apart: 9, of which 6 were waited for; matrix products, arithmetic and copies ran while one was open for 1% of the time, Pallas kernels for 3%

profile of v4, /device:TPU:0, one launch (start us, length us, event | category | flops | bytes accessed | tf_op | source)
XLA Modules:
  0.0 30.4 jit_solution(7357945631714648305)
XLA Ops:
  0.0 4.1 %collective-permute-start = (bf16[1,128,128]{2,1,0:T(8,128)(2,1)}, bf16[1,128,128]{2,1,0:T(8,128)(2,1)S(1)}, u32[]{:S(2)}, u32[]{:S(2)}) collective-permute-start(bf16[1,128,128]{2,1,0:T(8,128)(2,1)} %bitcast.12), channel_id=1, source_target_pairs={{0,4},{1,5},{2,6},{3,7},{4,0},{5,1},{6,2},{7,3},{8,12},{9,13},{10,... | collective-permute-start | bytes 98312 | tf_op jit(solution)/shard_map/ppermute | solution.py:39
  4.1 0.0 copy-start
  4.1 1.5 %collective-permute-start.3 = (bf16[1,128,256]{2,1,0:T(8,128)(2,1)}, bf16[1,128,256]{2,1,0:T(8,128)(2,1)S(1)}, u32[]{:S(2)}, u32[]{:S(2)}) collective-permute-start(bf16[1,128,256]{2,1,0:T(8,128)(2,1)} %bitcast.10), channel_id=1, source_target_pairs={{0,16},{8,24},{16,0},{24,8},{1,17},{9,25},{17,1},{25,9},{2,18},{10... | collective-permute-start | bytes 196616 | tf_op jit(solution)/shard_map/ppermute | solution.py:39
  5.6 0.0 copy-start.1
  5.6 0.8 %copy-done.1 = bf16[1,4,32,128]{3,2,1,0:T(8,128)(2,1)S(1)} copy-done((bf16[1,4,32,128]{3,2,1,0:T(8,128)(2,1)S(1)}, bf16[1,4,32,128]{3,2,1,0:T(8,128)(2,1)}, u32[]{:S(2)}) %copy-start.1) | copy-done | bytes 32792
  6.3 0.0 copy-done
  6.4 0.0 copy-start.6
  6.4 0.1 collective-permute-done.refs_1_
  6.5 1.6 %collective-permute-start.1 = (bf16[2,128,128]{2,1,0:T(8,128)(2,1)S(1)}, bf16[2,128,128]{2,1,0:T(8,128)(2,1)S(1)}, u32[]{:S(2)}, u32[]{:S(2)}) collective-permute-start(bf16[2,128,128]{2,1,0:T(8,128)(2,1)S(1)} %pad_maximum_fusion.2), channel_id=1, source_target_pairs={{0,2},{1,3},{2,0},{3,1},{4,6},{5,7},{6,4},{7,5},{8,10},{9,11},{10,... | collective-permute-start | bytes 196616 | tf_op jit(solution)/shard_map/ppermute | solution.py:39
  8.2 0.4 %collective-permute-done.3.refs_5_ = bf16[1,128,256]{2,1,0:T(8,128)(2,1)S(1)} collective-permute-done((bf16[1,128,256]{2,1,0:T(8,128)(2,1)}, bf16[1,128,256]{2,1,0:T(8,128)(2,1)S(1)}, u32[]{:S(2)}, u32[]{:S(2)}) %collective-permute-start.3) | collective-permute-done | bytes 65568 | tf_op jit(solution)/shard_map/ppermute | solution.py:39
  8.6 1.6 %collective-permute-start.4 = (bf16[2,128,256]{2,1,0:T(8,128)(2,1)S(1)}, bf16[2,128,256]{2,1,0:T(8,128)(2,1)S(1)}, u32[]{:S(2)}, u32[]{:S(2)}) collective-permute-start(bf16[2,128,256]{2,1,0:T(8,128)(2,1)S(1)} %pad_maximum_fusion.1), channel_id=1, source_target_pairs={{0,8},{8,0},{16,24},{24,16},{1,9},{9,1},{17,25},{25,17},{2,10},{10... | collective-permute-start | bytes 393224 | tf_op jit(solution)/shard_map/ppermute | solution.py:39
  10.1 0.7 %collective-permute-done.1.refs_2_ = bf16[2,128,128]{2,1,0:T(8,128)(2,1)S(1)} collective-permute-done((bf16[2,128,128]{2,1,0:T(8,128)(2,1)S(1)}, bf16[2,128,128]{2,1,0:T(8,128)(2,1)S(1)}, u32[]{:S(2)}, u32[]{:S(2)}) %collective-permute-start.1) | collective-permute-done | bytes 65568 | tf_op jit(solution)/shard_map/ppermute | solution.py:39
  10.9 0.1 collective-permute-start.2
  11.6 0.0 copy-done.6
  11.6 0.2 copy.9
  11.8 1.8 %collective-permute-done.4.refs_6_ = bf16[2,128,256]{2,1,0:T(8,128)(2,1)S(1)} collective-permute-done((bf16[2,128,256]{2,1,0:T(8,128)(2,1)S(1)}, bf16[2,128,256]{2,1,0:T(8,128)(2,1)S(1)}, u32[]{:S(2)}, u32[]{:S(2)}) %collective-permute-start.4) | collective-permute-done | bytes 131104 | tf_op jit(solution)/shard_map/ppermute | solution.py:39
  13.6 0.0 collective-permute-done.2.refs_3_
  13.6 0.6 %volume.1 = (bf16[4,4,8,128]{3,2,1,0:T(8,128)(2,1)S(1)}, bf16[3,4,8,128]{3,2,1,0:T(8,128)(2,1)S(1)}, bf16[3,4,8,128]{3,2,1,0:T(8,128)(2,1)S(1)}) custom-call(bf16[1,128,128]{2,1,0:T(8,128)(2,1)S(1)} %own.2.refs_0_, bf16[1,128,128]{2,1,0:T(8,128)(2,1)S(1)} %collective-permute-done.refs_1_, bf16[2,128,128]{2,1,0:T(8,128)(2,1)S(1)} %collective-permute-done.1.refs_2_, ...), custom_call_target="tpu_custom_call" | custom-call | tf_op jit(solution)/shard_map/volume/pallas_call | solution.py:444
  14.2 1.5 %collective-permute-start.5 = (bf16[3,4,8,128]{3,2,1,0:T(8,128)(2,1)S(1)}, bf16[3,4,8,128]{3,2,1,0:T(8,128)(2,1)S(1)}, u32[]{:S(2)}, u32[]{:S(2)}) collective-permute-start(bf16[3,4,8,128]{3,2,1,0:T(8,128)(2,1)S(1)} %get-tuple-element.14), channel_id=1, source_target_pairs={{0,8},{8,16},{16,24},{24,0},{1,9},{9,17},{17,25},{25,1},{2,10},{10... | collective-permute-start | bytes 73736 | tf_op jit(solution)/shard_map/ppermute | solution.py:57
  15.8 1.4 %collective-permute-start.6 = (bf16[3,4,8,128]{3,2,1,0:T(8,128)(2,1)S(1)}, bf16[3,4,8,128]{3,2,1,0:T(8,128)(2,1)S(1)}, u32[]{:S(2)}, u32[]{:S(2)}) collective-permute-start(bf16[3,4,8,128]{3,2,1,0:T(8,128)(2,1)S(1)} %get-tuple-element.15), channel_id=1, source_target_pairs={{8,0},{16,8},{24,16},{0,24},{9,1},{17,9},{25,17},{1,25},{10,2},{18... | collective-permute-start | bytes 73736 | tf_op jit(solution)/shard_map/ppermute | solution.py:57
  17.2 2.4 %collective-permute-done.6.high_a_ref = bf16[3,4,8,128]{3,2,1,0:T(8,128)(2,1)S(1)} collective-permute-done((bf16[3,4,8,128]{3,2,1,0:T(8,128)(2,1)S(1)}, bf16[3,4,8,128]{3,2,1,0:T(8,128)(2,1)S(1)}, u32[]{:S(2)}, u32[]{:S(2)}) %collective-permute-start.6) | collective-permute-done | bytes 24608 | tf_op jit(solution)/shard_map/ppermute | solution.py:57
  19.6 0.0 collective-permute-done.5.low_a_ref
  19.6 0.1 collective-permute-start.7
  19.7 0.0 copy-start.2
  19.7 0.0 copy-start.3
  19.8 3.6 %collective-permute-start.8 = (bf16[10,3,8,128]{3,2,1,0:T(8,128)(2,1)S(1)}, bf16[10,3,8,128]{3,2,1,0:T(8,128)(2,1)S(1)}, u32[]{:S(2)}, u32[]{:S(2)}) collective-permute-start(bf16[10,3,8,128]{3,2,1,0:T(8,128)(2,1)S(1)} %pad_maximum_fusion.4), channel_id=1, source_target_pairs={{1,0},{2,1},{3,2},{4,3},{5,4},{6,5},{7,6},{0,7},{9,8},{10,9},{11,1... | collective-permute-start | bytes 184328 | tf_op jit(solution)/shard_map/ppermute | solution.py:57
  23.3 0.0 copy-start.4
  23.3 0.0 copy-start.5
  23.3 0.0 copy-done.2
  23.3 0.0 copy-done.3
  23.3 0.6 %copy-done.4 = f32[16]{0:T(128)S(1)} copy-done((f32[16]{0:T(128)S(1)}, f32[16]{0:T(128)}, u32[]{:S(2)}) %copy-start.4) | copy-done | bytes 88
  24.0 0.0 copy-done.5
  24.0 1.0 %weights.1 = (f32[3,16,128]{2,1,0:T(8,128)S(1)}, bf16[256,256]{1,0:T(8,128)(2,1)S(1)}, bf16[192,768]{1,0:T(8,128)(2,1)S(1)}, bf16[144,768]{1,0:T(8,128)(2,1)S(1)}) custom-call(f32[16]{0:T(128)S(1)} %copy-done.4, f32[16]{0:T(128)S(1)} %copy-done.5, f32[1]{0:T(128)S(6)} %copy.10.b3_ref, bf16[27,3,16]{2,1,0:T(4,128)(2,1)S(1)} %bitcast.14, ...), custom_call_target="tpu_custom_call" | custom-call | flops 2000000000 | bytes 1000000 | tf_op jit(solution)/shard_map/weights/pallas_call | solution.py:417
  25.0 0.2 collective-permute-done.7.low_b_ref
  25.2 0.0 collective-permute-done.8.high_b_ref
  25.2 5.2 %layers.1 = bf16[4,4,32,32]{3,2,1,0:T(8,128)(2,1)} custom-call(f32[3,16,128]{2,1,0:T(8,128)S(1)} %get-tuple-element.12.bias_ref, bf16[4,4,8,128]{3,2,1,0:T(8,128)(2,1)S(1)} %get-tuple-element.13.own_ref, bf16[3,4,8,128]{3,2,1,0:T(8,128)(2,1)S(1)} %collective-permute-done.5.low_a_ref, bf16[3,4,8,128]{3,2,1,0:T(8,128)(2,1)S(1)} %collective-permute-done.6.high_a_ref, ...), custom_call_target="tpu_custom_call" | custom-call | tf_op jit(solution)/shard_map/layers/pallas_call | solution.py:466
  (10 shorter events, 0.1 us)
Async XLA Ops:
  0.0 6.5 %collective-permute-start = (bf16[1,128,128]{2,1,0:T(8,128)(2,1)}, bf16[1,128,128]{2,1,0:T(8,128)(2,1)S(1)}, u32[]{:S(2)}, u32[]{:S(2)}) collective-permute-start(bf16[1,128,128]{2,1,0:T(8,128)(2,1)} %bitcast.12), channel_id=1, source_target_pairs={{0,4},{1,5},{2,6},{3,7},{4,0},{5,1},{6,2},{7,3},{8,12},{9,13},{10,... | collective-permute-start | bytes 98312 | tf_op jit(solution)/shard_map/ppermute | solution.py:39
  4.1 2.3 %copy-start = (bf16[1,4,32,256]{3,2,1,0:T(8,128)(2,1)S(1)}, bf16[1,4,32,256]{3,2,1,0:T(8,128)(2,1)}, u32[]{:S(2)}) copy-start(bf16[1,4,32,256]{3,2,1,0:T(8,128)(2,1)} %param.9) | copy-start | bytes 196612
  4.1 4.5 %collective-permute-start.3 = (bf16[1,128,256]{2,1,0:T(8,128)(2,1)}, bf16[1,128,256]{2,1,0:T(8,128)(2,1)S(1)}, u32[]{:S(2)}, u32[]{:S(2)}) collective-permute-start(bf16[1,128,256]{2,1,0:T(8,128)(2,1)} %bitcast.10), channel_id=1, source_target_pairs={{0,16},{8,24},{16,0},{24,8},{1,17},{9,25},{17,1},{25,9},{2,18},{10... | collective-permute-start | bytes 196616 | tf_op jit(solution)/shard_map/ppermute | solution.py:39
  5.6 0.8 %copy-start.1 = (bf16[1,4,32,128]{3,2,1,0:T(8,128)(2,1)S(1)}, bf16[1,4,32,128]{3,2,1,0:T(8,128)(2,1)}, u32[]{:S(2)}) copy-start(bf16[1,4,32,128]{3,2,1,0:T(8,128)(2,1)} %param.8) | copy-start | bytes 98308
  6.4 5.2 %copy-start.6 = (bf16[3,3,3,3,16,16]{5,4,3,2,1,0:T(8,128)(2,1)S(1)}, bf16[3,3,3,3,16,16]{5,4,3,2,1,0:T(8,128)(2,1)}, u32[]{:S(2)}) copy-start(bf16[3,3,3,3,16,16]{5,4,3,2,1,0:T(8,128)(2,1)} %param.12) | copy-start | bytes 124420
  6.5 4.3 %collective-permute-start.1 = (bf16[2,128,128]{2,1,0:T(8,128)(2,1)S(1)}, bf16[2,128,128]{2,1,0:T(8,128)(2,1)S(1)}, u32[]{:S(2)}, u32[]{:S(2)}) collective-permute-start(bf16[2,128,128]{2,1,0:T(8,128)(2,1)S(1)} %pad_maximum_fusion.2), channel_id=1, source_target_pairs={{0,2},{1,3},{2,0},{3,1},{4,6},{5,7},{6,4},{7,5},{8,10},{9,11},{10,... | collective-permute-start | bytes 196616 | tf_op jit(solution)/shard_map/ppermute | solution.py:39
  8.6 5.0 %collective-permute-start.4 = (bf16[2,128,256]{2,1,0:T(8,128)(2,1)S(1)}, bf16[2,128,256]{2,1,0:T(8,128)(2,1)S(1)}, u32[]{:S(2)}, u32[]{:S(2)}) collective-permute-start(bf16[2,128,256]{2,1,0:T(8,128)(2,1)S(1)} %pad_maximum_fusion.1), channel_id=1, source_target_pairs={{0,8},{8,0},{16,24},{24,16},{1,9},{9,1},{17,25},{25,17},{2,10},{10... | collective-permute-start | bytes 393224 | tf_op jit(solution)/shard_map/ppermute | solution.py:39
  10.9 2.7 %collective-permute-start.2 = (bf16[4,128,128]{2,1,0:T(8,128)(2,1)S(1)}, bf16[4,128,128]{2,1,0:T(8,128)(2,1)S(1)}, u32[]{:S(2)}, u32[]{:S(2)}) collective-permute-start(bf16[4,128,128]{2,1,0:T(8,128)(2,1)S(1)} %pad_maximum_fusion), channel_id=1, source_target_pairs={{0,1},{1,0},{2,3},{3,2},{4,5},{5,4},{6,7},{7,6},{8,9},{9,8},{10,11... | collective-permute-start | bytes 393224 | tf_op jit(solution)/shard_map/ppermute | solution.py:39
  14.2 5.4 %collective-permute-start.5 = (bf16[3,4,8,128]{3,2,1,0:T(8,128)(2,1)S(1)}, bf16[3,4,8,128]{3,2,1,0:T(8,128)(2,1)S(1)}, u32[]{:S(2)}, u32[]{:S(2)}) collective-permute-start(bf16[3,4,8,128]{3,2,1,0:T(8,128)(2,1)S(1)} %get-tuple-element.14), channel_id=1, source_target_pairs={{0,8},{8,16},{16,24},{24,0},{1,9},{9,17},{17,25},{25,1},{2,10},{10... | collective-permute-start | bytes 73736 | tf_op jit(solution)/shard_map/ppermute | solution.py:57
  15.8 3.8 %collective-permute-start.6 = (bf16[3,4,8,128]{3,2,1,0:T(8,128)(2,1)S(1)}, bf16[3,4,8,128]{3,2,1,0:T(8,128)(2,1)S(1)}, u32[]{:S(2)}, u32[]{:S(2)}) collective-permute-start(bf16[3,4,8,128]{3,2,1,0:T(8,128)(2,1)S(1)} %get-tuple-element.15), channel_id=1, source_target_pairs={{8,0},{16,8},{24,16},{0,24},{9,1},{17,9},{25,17},{1,25},{10,2},{18... | collective-permute-start | bytes 73736 | tf_op jit(solution)/shard_map/ppermute | solution.py:57
  19.6 5.6 %collective-permute-start.7 = (bf16[10,3,8,128]{3,2,1,0:T(8,128)(2,1)S(1)}, bf16[10,3,8,128]{3,2,1,0:T(8,128)(2,1)S(1)}, u32[]{:S(2)}, u32[]{:S(2)}) collective-permute-start(bf16[10,3,8,128]{3,2,1,0:T(8,128)(2,1)S(1)} %pad_maximum_fusion.3), channel_id=1, source_target_pairs={{0,1},{1,2},{2,3},{3,4},{4,5},{5,6},{6,7},{7,0},{8,9},{9,10},{10,1... | collective-permute-start | bytes 184328 | tf_op jit(solution)/shard_map/ppermute | solution.py:57
  19.7 3.6 %copy-start.2 = (bf16[3,3,3,3,1,16]{5,3,4,2,1,0:T(4,128)(2,1)S(1)}, bf16[3,3,3,3,1,16]{5,3,4,2,1,0:T(4,128)(2,1)}, u32[]{:S(2)}) copy-start(bf16[3,3,3,3,1,16]{5,3,4,2,1,0:T(4,128)(2,1)} %param.10) | copy-start | bytes 7780
  19.7 3.6 %copy-start.3 = (bf16[3,3,3,3,16,1]{4,3,5,2,1,0:T(4,128)(2,1)S(1)}, bf16[3,3,3,3,16,1]{4,3,5,2,1,0:T(4,128)(2,1)}, u32[]{:S(2)}) copy-start(bf16[3,3,3,3,16,1]{4,3,5,2,1,0:T(4,128)(2,1)} %param.14) | copy-start | bytes 7780
  19.8 5.4 %collective-permute-start.8 = (bf16[10,3,8,128]{3,2,1,0:T(8,128)(2,1)S(1)}, bf16[10,3,8,128]{3,2,1,0:T(8,128)(2,1)S(1)}, u32[]{:S(2)}, u32[]{:S(2)}) collective-permute-start(bf16[10,3,8,128]{3,2,1,0:T(8,128)(2,1)S(1)} %pad_maximum_fusion.4), channel_id=1, source_target_pairs={{1,0},{2,1},{3,2},{4,3},{5,4},{6,5},{7,6},{0,7},{9,8},{10,9},{11,1... | collective-permute-start | bytes 184328 | tf_op jit(solution)/shard_map/ppermute | solution.py:57
  23.3 0.7 %copy-start.4 = (f32[16]{0:T(128)S(1)}, f32[16]{0:T(128)}, u32[]{:S(2)}) copy-start(f32[16]{0:T(128)} %b1_ref.1) | copy-start | bytes 196
  23.3 0.7 %copy-start.5 = (f32[16]{0:T(128)S(1)}, f32[16]{0:T(128)}, u32[]{:S(2)}) copy-start(f32[16]{0:T(128)} %b2_ref.1) | copy-start | bytes 196
